TPU v7x, 128 devices: a whole 4x4x4 slice. The times are simulated.
128 devices in a mesh: dp: 16 (over z, x), mp: 8 (over y, core).
Axes of the slice: x: 4, y: 4, z: 4, core: 2. Of those that a mesh axis runs over, the one named last changes fastest.
Arguments:
- hash_codes: int32 [16384, 2048], P('dp'), may hold values from 0 to 32703, as said below
- w_hash: bfloat16 [2048, 8192], P(None, 'mp'), may hold values from -0.125 to 0.125
- norm_gain: float32 [8192], P('mp'), may hold values from 0.1 to 1.9
- norm_bias: float32 [8192], P('mp'), may hold values from -3 to 3
- w_out: bfloat16 [8192, 256], P('mp'), may hold values from -0.0625 to 0.0625
- dense_vectors: bfloat16 [16384, 8, 256], P('dp'), may hold values from -6 to 6
- field_mix: float32 [8], replicated, may hold values from -3 to 3
- labels: int32 [16384], P('dp'), may hold values 0 or 1
Outputs:
- grad_hash: float32 [2048, 8192], P('dp', 'mp')
- grad_gain: float32 [8192], P('mp')
- grad_bias: float32 [8192], P('mp')
- grad_out: float32 [8192, 256], P('mp')
- mean_loss: float32 [], replicated
Inputs may be any that keep to these rules, and one draw needn't show every extreme that they name: `hash_codes`: codes of fixed universal hashes of each id.
All inputs are finite; a program needn't handle non-finite values. No bound on the sum of `labels` on one device may be relied on, other than what follows from the above.
Results may differ from a plain program's by a relative error of at most 0.011.
Values may be sent and summed in bfloat16 or wider, within the bound.
No kernel may reach another device: no remote copies, remote signals or barrier semaphores. Data moves between devices by JAX's collectives and lax.ppermute only.
A program may use at most 192 MiB of HBM per device.

v0:
```python
import functools
import math

import jax
import jax.numpy as jnp
from jax import lax
from jax.experimental import pallas as pl
from jax.experimental.pallas import tpu as pltpu
from jax.sharding import Mesh
from jax.sharding import PartitionSpec as P


DP = ("z", "x")
MP = ("y", "core")
buckets = 32704.0
epsilon = 1e-05
grad_scale = 32.0
EXP_TOP = 20.0
LANES = 128
F32 = jnp.float32
BF16 = jnp.bfloat16
MIB = 1024 * 1024


def hop(value, axis, step):
    count = lax.axis_size(axis)
    return lax.ppermute(value, axis, [(i, (i + step) % count) for i in range(count)])


def exchange(blocks, axes):
    return lax.all_to_all(blocks, axes, 0, 0, tiled=True)


def call(body, ins, outs, scratch=(), flops=0, limit=16):
    place = {"v": pltpu.VMEM, "h": pltpu.HBM, "a": pl.ANY, "s": pltpu.SMEM, "p": pltpu.VMEM}
    held = {"p": pltpu.VMEM, "h": pltpu.HBM}
    arrays = [pltpu.with_memory_space_constraint(a, held[s]) if s in held else a for a, s in ins]
    shapes = [
        held[s](shape, dtype) if s in held else jax.ShapeDtypeStruct(shape, dtype) for shape, dtype, s in outs
    ]
    return pl.pallas_call(
        body,
        out_shape=shapes,
        in_specs=[pl.BlockSpec(memory_space=place[s]) for _, s in ins],
        out_specs=[pl.BlockSpec(memory_space=place[s]) for _, _, s in outs],
        scratch_shapes=list(scratch),
        cost_estimate=pl.CostEstimate(flops=flops, bytes_accessed=0, transcendentals=0),
        compiler_params=pltpu.CompilerParams(vmem_limit_bytes=limit * MIB),
    )(*arrays)


def dot(a, b):
    return jnp.dot(a, b, preferred_element_type=F32)


def span(i, size):
    return pl.ds(pl.multiple_of(i * size, size), size)


def rows_in(hbm, held, sems, k, i, size):
    at = span(i, size)
    return pltpu.make_async_copy(hbm.at[at, :], held.at[at, :], sems.at[k, i])


def as_inputs(codes):
    return (codes.astype(F32) * (2.0 / (buckets - 1.0)) - 1.0).astype(BF16)


def decode_body(codes_hbm, w_hbm, hidden_hbm, slope_hbm, sums, codes, weights, hidden, slope, inputs, pre_a, pre_b, totals,
                code_sem, w_sem, out_sem):
    rows, units = hidden.shape
    block, tile = pre_a.shape
    blocks, tiles = rows // block, units // tile
    pres = (pre_a, pre_b)
    part, strip = 32, 256

    def fetch(i):
        at = slice(i * block, (i + 1) * block)
        return pltpu.make_async_copy(codes_hbm.at[at, :], codes.at[at, :], code_sem.at[i])

    def fetch_w(n):
        cols = pl.ds(n * tile, tile)
        return pltpu.make_async_copy(w_hbm.at[:, cols], weights.at[:, cols], w_sem.at[n])

    def put(k, i):
        held, hbm = ((hidden, hidden_hbm), (slope, slope_hbm))[k]
        at = slice(i * block, (i + 1) * block)
        return pltpu.make_async_copy(held.at[at, :], hbm.at[at, :], out_sem.at[k, i])

    fetch(0).start()
    fetch_w(0).start()
    fetch_w(1).start()
    for i in range(1, blocks):
        fetch(i).start()
    totals[...] = jnp.zeros_like(totals)

    def convert(i):
        fetch(i).wait()
        for r in range(block // part):
            at = slice(i * block + r * part, i * block + (r + 1) * part)
            inputs[at, :] = as_inputs(codes[at, :])

    def finish(i, n):
        for c in range(tile // strip):
            cols = slice(n * tile + c * strip, n * tile + (c + 1) * strip)
            first = jnp.zeros((8, strip), F32)
            second = jnp.zeros((8, strip), F32)
            for r in range(block // part):
                at = slice(i * block + r * part, i * block + (r + 1) * part)
                x = pres[n][r * part : (r + 1) * part, c * strip : (c + 1) * strip]
                grown = jnp.exp(jnp.minimum(x, EXP_TOP))
                both = grown * (grown + 2.0)
                inverse = 1.0 / (both + 2.0)
                tangent = both * inverse
                value = x * tangent
                hidden[at, cols] = value
                slope[at, cols] = (tangent + (x * (4.0 * inverse)) * ((grown + grown * grown) * inverse)).astype(BF16)
                first = first + value.reshape(part // 8, 8, strip).sum(0)
                second = second + (value * value).reshape(part // 8, 8, strip).sum(0)
            totals[0:8, cols] += first
            totals[8:16, cols] += second

    convert(0)
    last = None
    for i in range(blocks):
        at = slice(i * block, (i + 1) * block)
        for n in range(tiles):
            if i == 0:
                fetch_w(n).wait()
            if n == tiles - 1 and i + 1 < blocks:
                convert(i + 1)
            pres[n][...] = dot(inputs[at, :], weights[:, n * tile : (n + 1) * tile])
            if last is not None:
                finish(*last)
                if last[1] == tiles - 1:
                    put(0, last[0]).start()
                    put(1, last[0]).start()
            last = (i, n)
    finish(*last)
    put(0, blocks - 1).start()
    put(1, blocks - 1).start()
    first = jnp.sum(totals[0:8, :], 0, keepdims=True)
    second = jnp.sum(totals[8:16, :], 0, keepdims=True)
    for k in range(sums.shape[0]):
        sums[k, 0:1, :] = first
        sums[k, 1:2, :] = second
    for i in range(blocks):
        for k in range(2):
            put(k, i).wait()


def turn_body(codes_hbm, after, turned_hbm, codes, turned, sem, out_sem):
    del after
    rows = codes.shape[0]
    block = LANES
    blocks = rows // block

    def put(i):
        at = span(i, block)
        return pltpu.make_async_copy(turned.at[:, at], turned_hbm.at[:, at], out_sem.at[i])

    for i in range(blocks):
        rows_in(codes_hbm, codes, sem, 0, i, block).start()

    def step(i, carry):
        at = span(i, block)
        rows_in(codes_hbm, codes, sem, 0, i, block).wait()
        for q in range(codes.shape[1] // 256):
            cols = slice(q * 256, (q + 1) * 256)
            turned[cols, at] = as_inputs(codes[at, cols]).T
        put(i).start()
        return carry

    lax.fori_loop(0, blocks, step, 0)
    for i in range(blocks):
        put(i).wait()


def mix_body(after, dense_hbm, mix, w_out, spread_hbm, mixed_t, dense, mixed, spread, sem, out_sem):
    del after
    rows = spread.shape[0]
    block = 64
    deep = dense.shape[1]
    fields = deep // block
    pairs = rows // (2 * block)
    group = rows // 2

    def fetch(i):
        return pltpu.make_async_copy(dense_hbm.at[span(i, deep), :], dense.at[i], sem.at[i])

    def put(i):
        at = slice(i * group, (i + 1) * group)
        return pltpu.make_async_copy(spread.at[at, :], spread_hbm.at[at, :], out_sem.at[i])

    for i in range(2 * pairs):
        fetch(i).start()
    high = mix[...].astype(BF16)
    low = (mix[...] - high.astype(F32)).astype(BF16)
    owner = lax.broadcasted_iota(jnp.int32, (block, deep), 1) // fields
    mine = owner == lax.broadcasted_iota(jnp.int32, (block, deep), 0)
    picks = jnp.concatenate(
        [jnp.where(mine, high.astype(F32), 0.0), jnp.where(mine, low.astype(F32), 0.0)], 0
    ).astype(BF16)

    def step(i, carry):
        fetch(2 * i).wait()
        fetch(2 * i + 1).wait()
        even = dot(picks, dense[2 * i])
        odd = dot(picks, dense[2 * i + 1])
        both = jnp.concatenate([even[:block] + even[block:], odd[:block] + odd[block:]], 0)
        at = span(i, 2 * block)
        mixed_t[:, at] = both.T
        mixed[at, :] = both.astype(BF16)
        return carry

    for g in range(2):
        lax.fori_loop(g * pairs // 2, (g + 1) * pairs // 2, step, 0)
        at = slice(g * group, (g + 1) * group)
        spread[at, :] = lax.dot_general(
            mixed[at, :], w_out[...], (((1,), (1,)), ((), ())), preferred_element_type=F32
        ).astype(BF16)
        put(g).start()
    for g in range(2):
        put(g).wait()


def logit_body(total_rows, arrived, gain, bias, hidden_hbm, spread_hbm, coef, parts, hidden, spread, sem):
    rows, units = hidden.shape
    block = LANES
    blocks = rows // block

    for i in range(blocks):
        rows_in(hidden_hbm, hidden, sem, 0, i, block).start()
        rows_in(spread_hbm, spread, sem, 1, i, block).start()
    stats = jnp.sum(arrived[...], 0)
    mean = stats[0:1] / total_rows
    var = stats[1:2] / total_rows - mean * mean
    inv = lax.rsqrt(var + epsilon)
    coef[0:1, :] = gain[...] * inv
    coef[1:2, :] = bias[...]
    coef[2:3, :] = mean
    coef[3:4, :] = inv

    def step(i, carry):
        at = span(i, block)
        rows_in(hidden_hbm, hidden, sem, 0, i, block).wait()
        rows_in(spread_hbm, spread, sem, 1, i, block).wait()
        total = jnp.zeros((block, LANES), F32)
        for n in range(units // LANES):
            cols = slice(n * LANES, (n + 1) * LANES)
            value = (hidden[at, cols] - coef[2:3, cols]) * coef[0:1, cols] + coef[1:2, cols]
            total = total + value * spread[at, cols].astype(F32)
        line = jnp.sum(total.T, 0, keepdims=True)
        for k in range(parts.shape[0]):
            parts[k, pl.ds(i, 1), :] = line
        return carry

    lax.fori_loop(0, blocks, step, 0)


def column(line):
    return jnp.broadcast_to(line, (LANES, LANES)).T


def two_parts(value):
    high = value.astype(BF16)
    return high, (value - high.astype(F32)).astype(BF16)


def grad_body(total_rows, arrived, labels, hidden_hbm, spread_hbm, coef, mixed_t, grads, packed, hidden, spread,
              normed, weighted, totals, sem):
    rows, units = hidden.shape
    emb = mixed_t.shape[0]
    block = LANES
    blocks = rows // block
    own = packed.shape[0]
    share = units // own
    for i in range(blocks):
        rows_in(hidden_hbm, hidden, sem, 0, i, block).start()
        rows_in(spread_hbm, spread, sem, 1, i, block).start()
    logits = jnp.sum(arrived[...], 0)
    targets = labels[...]
    positive = jnp.maximum(logits, 0.0) + jnp.log1p(jnp.exp(-jnp.abs(logits)))
    loss = jnp.sum(positive - targets * logits, keepdims=True)
    grads[...] = (jax.nn.sigmoid(logits) - targets) * (grad_scale / math.sqrt(total_rows))
    for i in range(blocks):
        at = slice(i * block, (i + 1) * block)
        weighted[:, at] = (mixed_t[:, at] * grads[i : i + 1, :]).astype(BF16)
    totals[...] = jnp.zeros_like(totals)

    def step(i, carry):
        at = span(i, block)
        rows_in(hidden_hbm, hidden, sem, 0, i, block).wait()
        rows_in(spread_hbm, spread, sem, 1, i, block).wait()
        weight = column(grads[pl.ds(i, 1), :])
        for n in range(units // LANES):
            cols = slice(n * LANES, (n + 1) * LANES)
            part = weight * spread[at, cols].astype(F32)
            centred = hidden[at, cols] - coef[2:3, cols]
            normed[at, cols] = (centred * coef[0:1, cols] + coef[1:2, cols]).astype(BF16)
            product = part * centred
            totals[0:8, cols] += part.reshape(block // 8, 8, LANES).sum(0)
            totals[8:16, cols] += product.reshape(block // 8, 8, LANES).sum(0)
        return carry

    lax.fori_loop(0, blocks, step, 0)
    bias = jnp.sum(totals[0:8, :], 0, keepdims=True)
    gain = jnp.sum(totals[8:16, :], 0, keepdims=True) * coef[3:4, :]
    cuts = [slice(q * emb, (q + 1) * emb) for q in range(units // emb)]
    lines = jnp.concatenate([bias[:, c] for c in cuts] + [gain[:, c] for c in cuts], 0)
    spare = [v.astype(F32) for v in two_parts(jnp.broadcast_to(loss, (1, emb)))]
    extra = jnp.concatenate(spare + [jnp.zeros((6, emb), F32)], 0).astype(BF16)
    for p, block_of in enumerate((*two_parts(lines), extra)):
        for k in range(own):
            packed[k, share + 8 * p : share + 8 * p + 8, :] = block_of
    for n in range(units // 512):
        cols = slice(n * 512, (n + 1) * 512)
        out = dot(weighted[...], normed[:, cols]).T.astype(BF16)
        for k in range(512 // share):
            packed[n * (512 // share) + k, 0:share, :] = out[k * share : (k + 1) * share, :]


def ahead_body(chunks, grads, hidden_hbm, spread_hbm, slope_hbm, coef, turned_hbm, terms_hbm, hidden, spread, slope, plain,
               flat, tilted, left, terms, sem, left_sem, out_sem):
    rows, units = hidden.shape
    block = LANES
    blocks = rows // block
    quarter = left.shape[1]
    sub = quarter // 4
    wide = units // 2
    far = [pltpu.make_async_copy(turned_hbm.at[span(chunks[2], quarter), :], left.at[0], left_sem.at[0])]
    for q in range(4):
        at = pl.ds(pl.multiple_of(q * quarter + chunks[6] * sub, sub), sub)
        far.append(pltpu.make_async_copy(turned_hbm.at[at, :], left.at[1, q * sub : (q + 1) * sub, :], left_sem.at[1 + q]))
    for i in range(blocks):
        rows_in(hidden_hbm, hidden, sem, 0, i, block).start()
        rows_in(spread_hbm, spread, sem, 1, i, block).start()
        rows_in(slope_hbm, slope, sem, 2, i, block).start()
    for copy in far:
        copy.start()

    def step(i, carry):
        at = span(i, block)
        rows_in(hidden_hbm, hidden, sem, 0, i, block).wait()
        rows_in(spread_hbm, spread, sem, 1, i, block).wait()
        rows_in(slope_hbm, slope, sem, 2, i, block).wait()
        weight = column(grads[pl.ds(i, 1), :])
        for n in range(units // LANES):
            cols = slice(n * LANES, (n + 1) * LANES)
            factor = coef[0:1, cols] * slope[at, cols].astype(F32)
            flat[at, cols] = factor.astype(BF16)
            plain[at, cols] = (factor * (weight * spread[at, cols].astype(F32))).astype(BF16)
            tilted[at, cols] = (factor * (hidden[at, cols] - coef[2:3, cols])).astype(BF16)
        return carry

    lax.fori_loop(0, blocks, step, 0)
    for copy in far:
        copy.wait()

    def put(k):
        return pltpu.make_async_copy(terms.at[k], terms_hbm.at[k], out_sem.at[k])

    for axis in range(2):
        cols = slice(axis * wide, (axis + 1) * wide)
        for k, right in enumerate((plain, flat, tilted)):
            terms[3 * axis + k] = dot(left[axis], right[:, cols]).astype(BF16)
            put(3 * axis + k).start()
    for k in range(6):
        put(k).wait()


def far_body(total_rows, arrived, coef, terms_hbm, z_hbm, x_hbm, both, grad_gain, grad_bias, loss, piece, terms, held, sem,
             out_sem):
    units = coef.shape[1]
    share, emb = piece.shape
    quarter, wide = terms.shape[1:]
    some = held.shape[1] - quarter

    def get(k):
        return pltpu.make_async_copy(terms_hbm.at[k], terms.at[k], sem.at[k])

    def put(axis):
        return pltpu.make_async_copy(held.at[axis], (z_hbm, x_hbm)[axis], out_sem.at[axis])

    for k in range(6):
        get(k).start()
    count = units // emb

    def stat(p):
        return jnp.sum(arrived[:, share + 8 * p : share + 8 * p + 8, :].astype(F32), 0)

    lines = stat(1) + stat(0)
    for q in range(count):
        cols = slice(q * emb, (q + 1) * emb)
        grad_bias[:, cols] = lines[q : q + 1]
        grad_gain[:, cols] = lines[count + q : count + q + 1]
        both[0:1, cols] = lines[q : q + 1] / total_rows
        both[1:2, cols] = lines[count + q : count + q + 1] * coef[3:4, cols] / total_rows
    loss[...] = jnp.sum(stat(2), 0, keepdims=True)[:, 0:LANES] / total_rows
    piece[...] = jnp.sum(arrived[:, 0:share, :].astype(F32), 0).astype(BF16)
    for axis in range(2):
        first = axis * 2 * some
        for n in range(2):
            held[axis, quarter:, n * 256 : (n + 1) * 256] = piece[first + n * some : first + (n + 1) * some, :]
        for k in range(3):
            get(3 * axis + k).wait()
        for r in range(quarter // LANES):
            at = slice(r * LANES, (r + 1) * LANES)
            for n in range(wide // LANES):
                cols = slice(n * LANES, (n + 1) * LANES)
                here = slice(axis * wide + n * LANES, axis * wide + (n + 1) * LANES)
                value = terms[3 * axis, at, cols].astype(F32) - terms[3 * axis + 1, at, cols].astype(F32) * both[0:1, here]
                value = value - terms[3 * axis + 2, at, cols].astype(F32) * both[1:2, here]
                held[axis, at, cols] = value.astype(BF16)
        put(axis).start()
    for axis in range(2):
        put(axis).wait()


def back_body(grads, hidden_hbm, spread_hbm, slope_hbm, coef, both, grad_pre, hidden, spread, slope, sem):
    rows, units = hidden.shape
    block = LANES
    blocks = rows // block
    for i in range(blocks):
        rows_in(hidden_hbm, hidden, sem, 0, i, block).start()
        rows_in(spread_hbm, spread, sem, 1, i, block).start()
        rows_in(slope_hbm, slope, sem, 2, i, block).start()

    def step(i, carry):
        at = span(i, block)
        rows_in(hidden_hbm, hidden, sem, 0, i, block).wait()
        rows_in(spread_hbm, spread, sem, 1, i, block).wait()
        rows_in(slope_hbm, slope, sem, 2, i, block).wait()
        weight = column(grads[pl.ds(i, 1), :])
        for n in range(units // LANES):
            cols = slice(n * LANES, (n + 1) * LANES)
            inner = weight * spread[at, cols].astype(F32) - both[0:1, cols]
            inner = inner - (hidden[at, cols] - coef[2:3, cols]) * both[1:2, cols]
            grad_pre[at, cols] = (inner * coef[0:1, cols] * slope[at, cols].astype(F32)).astype(BF16)
        return carry

    lax.fori_loop(0, blocks, step, 0)


def product_body(jobs, keep, chunks, turned, grad_pre, piece, after, *refs):
    del after
    count = len(jobs)
    outs, (lines, held, sem) = refs[:count], refs[count:]
    rows = lines.shape[0]
    wide = held.shape[2]
    some = held.shape[1] - rows
    sub = rows // 4

    def put(k):
        return pltpu.make_async_copy(held.at[k], outs[k], sem.at[k])

    for k, (axis, place) in enumerate(jobs):
        c = chunks[place]
        out = outs[k] if keep else held.at[k]
        if axis == "z":
            left = turned[span(c, rows), :]
            base, first = 0, 0
        else:
            for q in range(4):
                at = pl.ds(pl.multiple_of(q * rows + c * sub, sub), sub)
                lines[q * sub : (q + 1) * sub, :] = turned[at, :]
            left = lines[...]
            base, first = wide, 2 * some
        out[0:rows, :] = dot(left, grad_pre[:, base : base + wide]).astype(BF16)
        for n in range(2):
            out[rows:, n * 256 : (n + 1) * 256] = piece[first + n * some : first + (n + 1) * some, :]
        if not keep:
            put(k).start()
    if not keep:
        for k in range(count):
            put(k).wait()


def middle_body(chunk, own, far, up, down, own_out, far_out, up_out, down_out):
    me, was = chunk[0], chunk[1]
    rows = own_out.shape[0]
    full = own.shape[0] - (far_out.shape[0] - rows) // 4
    some = (far_out.shape[0] - rows) // 4
    for step, out in ((2, far_out), (1, up_out), (3, down_out), (0, own_out)):
        at = span(lax.rem(me + step, 4), rows)
        total = (own[at, :].astype(F32) + far[at, :].astype(F32)) + (up[at, :].astype(F32) + down[at, :].astype(F32))
        out[0:rows, :] = total.astype(out.dtype)
        if step:
            for back, came in ((0, own), (2, far), (1, up), (3, down)):
                to = pl.ds(pl.multiple_of(rows + lax.rem(was + 4 - back, 4) * some, some), some)
                out[to, :] = came[full:, :]


def last_body(place, own_a, a0, a2, a1, a3, own_b, b0, b2, b1, b3, hash_hbm, out_hbm, grad_hash, grad_out, sem):
    rows, half = own_a.shape
    some = (a0.shape[0] - rows) // 4
    share = 4 * some
    for kind, pieces in ((0, (a0, a2, a1, a3)), (1, (b0, b2, b1, b3))):
        me = place[1 - kind]
        for back, came in zip((0, 2, 1, 3), pieces):
            there = lax.rem(me + 4 - back, 4)
            for k in range(4):
                owner = k * 4 + there if kind == 0 else there * 4 + k
                for n in range(2):
                    to = pl.ds(pl.multiple_of(owner * share + (2 * kind + n) * some, some), some)
                    at = slice(rows + k * some, rows + (k + 1) * some)
                    grad_out[to, :] = came[at, n * 256 : (n + 1) * 256].astype(F32)
    put_out = pltpu.make_async_copy(grad_out, out_hbm, sem.at[0])
    put_out.start()
    for base, own, came in ((0, own_a, (a2, a1, a3)), (half, own_b, (b2, b1, b3))):
        total = own[...]
        for part in came:
            total = total + part[0:rows, :].astype(F32)
        grad_hash[:, base : base + half] = total
    put_hash = pltpu.make_async_copy(grad_hash, hash_hbm, sem.at[1])
    put_hash.start()
    put_out.wait()
    put_hash.wait()


def on_device(hash_codes, w_hash, norm_gain, norm_bias, w_out, dense_vectors, field_mix, labels):
    rows, codes = hash_codes.shape
    units = w_hash.shape[1]
    fields, emb = dense_vectors.shape[1:]
    dp, mp = lax.axis_size(DP), lax.axis_size(MP)
    total_rows = rows * dp
    lines = rows // LANES
    half = units // 2
    share = units // dp
    some = share // 4
    dma = pltpu.SemaphoreType.DMA
    hidden, slope, sums = call(
        decode_body,
        [(hash_codes, "h"), (w_hash, "h")],
        [((rows, units), F32, "h"), ((rows, units), BF16, "h"), ((dp, 2, units), F32, "v")],
        [
            pltpu.VMEM((rows, codes), jnp.int32),
            pltpu.VMEM((codes, units), BF16),
            pltpu.VMEM((rows, units), F32),
            pltpu.VMEM((rows, units), BF16),
            pltpu.VMEM((rows, codes), BF16),
            pltpu.VMEM((256, units // 2), F32),
            pltpu.VMEM((256, units // 2), F32),
            pltpu.VMEM((16, units), F32),
            dma((rows // 256,)),
            dma((2,)),
            dma((2, rows // 256)),
        ],
        flops=2 * rows * codes * units,
        limit=40,
    )
    arrived = exchange(sums, DP)
    mix_line = jnp.tile(field_mix / math.sqrt(emb), 64).reshape(1, fields * 64)
    spread, mixed_t = call(
        mix_body,
        [(sums, "h"), (dense_vectors.reshape(rows * fields, emb), "h"), (mix_line, "v"), (w_out, "v")],
        [((rows, units), BF16, "h"), ((emb, rows), F32, "v")],
        [
            pltpu.VMEM((rows // 64, fields * 64, emb), BF16),
            pltpu.VMEM((rows, emb), BF16),
            pltpu.VMEM((rows, units), BF16),
            dma((rows // 64,)),
            dma((2,)),
        ],
        flops=8 * rows * units * emb,
        limit=16,
    )
    coef, parts = call(
        functools.partial(logit_body, float(total_rows)),
        [
            (arrived, "v"),
            (norm_gain.reshape(1, units), "v"),
            (norm_bias.reshape(1, units), "v"),
            (hidden, "h"),
            (spread, "h"),
        ],
        [((8, units), F32, "v"), ((mp, lines, LANES), F32, "v")],
        [pltpu.VMEM((rows, units), F32), pltpu.VMEM((rows, units), BF16), dma((2, lines))],
        limit=20,
        flops=4 * rows * units,
    )
    logits = exchange(parts, MP)
    (turned,) = call(
        turn_body,
        [(hash_codes, "h"), (parts, "h")],
        [((codes, rows), BF16, "h")],
        [pltpu.VMEM((rows, codes), jnp.int32), pltpu.VMEM((codes, rows), BF16), dma((1, lines)), dma((lines,))],
        flops=16 * rows * codes * LANES,
        limit=16,
    )
    targets = labels.astype(F32).reshape(lines, LANES)
    grads, packed = call(
        functools.partial(grad_body, float(total_rows)),
        [(logits, "v"), (targets, "v"), (hidden, "h"), (spread, "h"), (coef, "v"), (mixed_t, "v")],
        [((lines, LANES), F32, "v"), ((dp, share + 24, emb), BF16, "v")],
        [
            pltpu.VMEM((rows, units), F32),
            pltpu.VMEM((rows, units), BF16),
            pltpu.VMEM((rows, units), BF16),
            pltpu.VMEM((emb, rows), BF16),
            pltpu.VMEM((16, units), F32),
            dma((2, lines)),
        ],
        limit=24,
        flops=2 * rows * units * emb,
    )
    grad_arrived = exchange(packed, DP)
    here = {axis: lax.axis_index(axis).astype(jnp.int32) for axis in DP}
    chunks = jnp.stack([(here[axis] + step) & 3 for axis in DP for step in range(4)])
    size = (codes // 4 + some, half)
    (terms,) = call(
        ahead_body,
        [
            (chunks, "s"),
            (grads, "v"),
            (hidden, "h"),
            (spread, "h"),
            (slope, "h"),
            (coef, "v"),
            (turned, "h"),
        ],
        [((6, codes // 4, half), BF16, "h")],
        [pltpu.VMEM((rows, units), F32)]
        + [pltpu.VMEM((rows, units), BF16)] * 5
        + [
            pltpu.VMEM((2, codes // 4, rows), BF16),
            pltpu.VMEM((6, codes // 4, half), BF16),
            dma((3, lines)),
            dma((5,)),
            dma((6,)),
        ],
        flops=6 * rows * half * codes,
        limit=30,
    )
    far_z, far_x, both, grad_gain, grad_bias, loss, piece = call(
        functools.partial(far_body, float(total_rows)),
        [(grad_arrived, "v"), (coef, "v"), (terms, "h")],
        [
            (size, BF16, "h"),
            (size, BF16, "h"),
            ((8, units), F32, "p"),
            ((1, units), F32, "v"),
            ((1, units), F32, "v"),
            ((1, LANES), F32, "v"),
            ((share, emb), BF16, "p"),
        ],
        [pltpu.VMEM((6, codes // 4, half), BF16), pltpu.VMEM((2, *size), BF16), dma((6,)), dma((2,))],
        limit=10,
        flops=8 * rows * units,
    )
    (grad_pre,) = call(
        back_body,
        [(grads, "v"), (hidden, "h"), (spread, "h"), (slope, "h"), (coef, "v"), (both, "p")],
        [((rows, units), BF16, "p")],
        [
            pltpu.VMEM((rows, units), F32),
            pltpu.VMEM((rows, units), BF16),
            pltpu.VMEM((rows, units), BF16),
            dma((3, lines)),
        ],
        limit=20,
        flops=8 * rows * units,
    )


    def products(steps, keep, after):
        jobs = [(axis, 4 * DP.index(axis) + step) for step in steps for axis in DP]
        outs = call(
            functools.partial(product_body, jobs, keep),
            [(chunks, "s"), (turned, "p"), (grad_pre, "p"), (piece, "p"), (after, "h")],
            [(size, BF16, "p" if keep else "h")] * len(jobs),
            [pltpu.VMEM((codes // 4, rows), BF16), pltpu.VMEM((1 if keep else len(jobs), *size), BF16), dma((len(jobs),))],
            flops=2 * rows * half * (codes // 4) * len(jobs),
            limit=8,
        )
        return {(axis, place & 3): out for (axis, place), out in zip(jobs, outs)}

    made = {("z", 2): far_z, ("x", 2): far_x}
    made.update(products((1,), False, terms))
    made.update(products((3,), False, made["z", 1]))
    made.update(products((0,), True, made["z", 3]))
    got = {(axis, step): hop(made[axis, step], axis, step) for step in (2, 1, 3) for axis in DP}
    other = {"z": "x", "x": "z"}
    last = []
    for axis in DP:
        own, far, up, down = call(
            middle_body,
            [(jnp.stack([here[other[axis]], here[axis]]), "s"), (made[axis, 0], "p")]
            + [(got[axis, step], "p") for step in (2, 1, 3)],
            [((codes // 16, half), F32, "p")] + [((codes // 16 + 4 * some, half), BF16, "p")] * 3,
            limit=4,
            flops=rows * units,
        )
        last += [own, far] + [hop(v, other[axis], step) for v, step in ((far, 2), (up, 1), (down, 3))]
    grad_hash, grad_out = call(
        last_body,
        [(jnp.stack([here["z"], here["x"]]), "s")] + [(v, "p") for v in last],
        [((codes // 16, units), F32, "h"), ((units, emb), F32, "h")],
        [pltpu.VMEM((codes // 16, units), F32), pltpu.VMEM((units, emb), F32), dma((2,))],
        limit=8,
        flops=rows * units,
    )
    return (grad_hash, grad_gain.reshape(units), grad_bias.reshape(units), grad_out, loss[0, 0])


def solution(mesh):
    split = Mesh(mesh.devices.reshape(4, 4, 4, 2), ("z", "x", "y", "core"))
    return jax.shard_map(
        on_device,
        mesh=split,
        in_specs=(P(DP, None), P(None, MP), P(MP), P(MP), P(MP, None), P(DP, None, None), P(), P(DP)),
        out_specs=(P(DP, MP), P(MP), P(MP), P(MP, None), P()),
        check_vma=False,
    )
```

profile of v0, /device:TPU:0, one launch (start us, length us, event | category | flops | bytes accessed | tf_op | source)
XLA Modules:
  0.0 130.2 jit_solution(11709326905535984218)
XLA Ops:
  0.7 12.8 %shard_map.119 = (f32[1024,1024]{1,0:T(8,128)}, bf16[1024,1024]{1,0:T(8,128)(2,1)}, f32[16,2,1024]{2,1,0:T(2,128)}) custom-call(s32[1024,2048]{1,0:T(8,128)} %codes_hbm.3, bf16[2048,1024]{1,0:T(8,128)(2,1)} %w_hbm.1), custom_call_target="tpu_custom_call" | custom-call | flops 4294967296 | tf_op jit(solution)/shard_map/pallas_call | solution.py:41
  13.5 8.0 %all-to-all-start = ((f32[16,2,1024]{2,1,0:T(2,128)}), f32[16,2,1024]{2,1,0:T(2,128)S(1)}, u32[]{:S(2)}, u32[]{:S(2)}) async-start(f32[16,2,1024]{2,1,0:T(2,128)} %get-tuple-element.37.after), calls=%async_computation | async-start | bytes 262144 | tf_op jit(solution)/shard_map/all_to_all | solution.py:31
  21.6 5.6 %shard_map.120 = (bf16[1024,1024]{1,0:T(8,128)(2,1)}, f32[256,1024]{1,0:T(8,128)S(1)}) custom-call(f32[16,2,1024]{2,1,0:T(2,128)} %get-tuple-element.37.after, bf16[8192,256]{1,0:T(8,128)(2,1)} %bitcast.21, f32[1,512]{1,0:T(1,128)S(1)} %reshape_tile.3.mix, bf16[1024,256]{1,0:T(8,128)(2,1)S(1)} %copy-done.3), custom_call_target="tpu_custom_call" | custom-call | flops 2147483648 | tf_op jit(solution)/shard_map/pallas_call | solution.py:41
  27.2 2.2 %all-to-all-done.arrived = f32[16,2,1024]{2,1,0:T(2,128)S(1)} async-done(((f32[16,2,1024]{2,1,0:T(2,128)}), f32[16,2,1024]{2,1,0:T(2,128)S(1)}, u32[]{:S(2)}, u32[]{:S(2)}) %all-to-all-start) | async-done | bytes 131104 | tf_op jit(solution)/shard_map/all_to_all | solution.py:31
  29.5 3.7 %shard_map.121 = (f32[8,1024]{1,0:T(8,128)S(1)}, f32[8,8,128]{2,1,0:T(8,128)}) custom-call(f32[16,2,1024]{2,1,0:T(2,128)S(1)} %all-to-all-done.arrived, f32[1,1024]{1,0:T(1,128)S(1)} %bitcast.19, f32[1,1024]{1,0:T(1,128)S(1)} %bitcast.20, f32[1024,1024]{1,0:T(8,128)} %get-tuple-element.38.hidden_hbm, bf16[1024,1024]{1,0:T(8,128)(2,1)} %get-tuple-element.39.spread_hbm), custom_call_target="tpu_custom_call" | custom-call | flops 4194304 | tf_op jit(solution)/shard_map/pallas_call | solution.py:41
  33.2 4.5 %all-to-all-start.1 = ((f32[8,8,128]{2,1,0:T(8,128)}), f32[8,8,128]{2,1,0:T(8,128)S(1)}, u32[]{:S(2)}, u32[]{:S(2)}) async-start(f32[8,8,128]{2,1,0:T(8,128)} %get-tuple-element.40.after), calls=%async_computation.1 | async-start | bytes 65536 | tf_op jit(solution)/shard_map/all_to_all | solution.py:31
  37.8 5.3 %all-to-all-done.1.arrived = f32[8,8,128]{2,1,0:T(8,128)S(1)} async-done(((f32[8,8,128]{2,1,0:T(8,128)}), f32[8,8,128]{2,1,0:T(8,128)S(1)}, u32[]{:S(2)}, u32[]{:S(2)}) %all-to-all-start.1) | async-done | bytes 32800 | tf_op jit(solution)/shard_map/all_to_all | solution.py:31
  43.1 4.7 %shard_map.123 = (f32[8,128]{1,0:T(8,128)S(1)}, bf16[16,88,256]{2,1,0:T(8,128)(2,1)}) custom-call(f32[8,8,128]{2,1,0:T(8,128)S(1)} %all-to-all-done.1.arrived, f32[8,128]{1,0:T(8,128)S(1)} %convert_bitcast_fusion.labels, f32[1024,1024]{1,0:T(8,128)} %get-tuple-element.38.hidden_hbm, bf16[1024,1024]{1,0:T(8,128)(2,1)} %get-tuple-element.39.spread_hbm, ...), custom_call_target="tpu_custom_call" | custom-call | flops 536870912 | tf_op jit(solution)/shard_map/pallas_call | solution.py:41
  47.8 5.0 %all-to-all-start.2 = ((bf16[16,88,256]{2,1,0:T(8,128)(2,1)}), bf16[16,88,256]{2,1,0:T(8,128)(2,1)S(1)}, u32[]{:S(2)}, u32[]{:S(2)}) async-start(bf16[16,88,256]{2,1,0:T(8,128)(2,1)} %get-tuple-element.45), calls=%async_computation.2 | async-start | bytes 1441792 | tf_op jit(solution)/shard_map/all_to_all | solution.py:31
  52.9 5.6 %shard_map.122.turned_hbm.turned = bf16[2048,1024]{1,0:T(8,128)(2,1)} custom-call(s32[1024,2048]{1,0:T(8,128)} %codes_hbm.3, f32[8,8,128]{2,1,0:T(8,128)} %get-tuple-element.40.after), custom_call_target="tpu_custom_call" | custom-call | flops 4294967296 | tf_op jit(solution)/shard_map/pallas_call | solution.py:41
  58.4 9.1 %shard_map.124.terms_hbm.after = bf16[6,512,512]{2,1,0:T(8,128)(2,1)} custom-call(s32[8]{0:T(128)S(1)} %stack.56.chunks, f32[8,128]{1,0:T(8,128)S(1)} %get-tuple-element.43.grads, f32[1024,1024]{1,0:T(8,128)} %get-tuple-element.38.hidden_hbm, bf16[1024,1024]{1,0:T(8,128)(2,1)} %get-tuple-element.39.spread_hbm, ...), custom_call_target="tpu_custom_call" | custom-call | flops 6442450944 | tf_op jit(solution)/shard_map/pallas_call | solution.py:41
  67.6 3.6 %shard_map.125 = (bf16[528,512]{1,0:T(8,128)(2,1)}, bf16[528,512]{1,0:T(8,128)(2,1)}, f32[8,1024]{1,0:T(8,128)S(1)}, f32[1,1024]{1,0:T(1,128)}, f32[1,1024]{1,0:...) custom-call(bf16[16,88,256]{2,1,0:T(8,128)(2,1)S(1)} %all-to-all-done.2.arrived, ...), custom_call_target="tpu_custom_call" | custom-call | flops 8388608 | tf_op jit(solution)/shard_map/pallas_call | solution.py:41
  71.2 3.9 %shard_map.126.grad_pre = bf16[1024,1024]{1,0:T(8,128)(2,1)S(1)} custom-call(f32[8,128]{1,0:T(8,128)S(1)} %get-tuple-element.43.grads, f32[1024,1024]{1,0:T(8,128)} %get-tuple-element.38.hidden_hbm, bf16[1024,1024]{1,0:T(8,128)(2,1)} %get-tuple-element.39.spread_hbm, bf16[1024,1024]{1,0:T(8,128)(2,1)} %get-tuple-element.44.slope_hbm, ...), custom_call_target="tpu_custom_call" | custom-call | flops 8388608 | tf_op jit(solution)/shard_map/pallas_call | solution.py:41
  75.8 2.6 %shard_map.127 = (bf16[528,512]{1,0:T(8,128)(2,1)}, bf16[528,512]{1,0:T(8,128)(2,1)}) custom-call(s32[8]{0:T(128)S(1)} %stack.56.chunks, bf16[2048,1024]{1,0:T(8,128)(2,1)S(1)} %copy-done, bf16[1024,1024]{1,0:T(8,128)(2,1)S(1)} %shard_map.126.grad_pre, bf16[64,256]{1,0:T(8,128)(2,1)S(1)} %get-tuple-element.47.piece, ...), custom_call_target="tpu_custom_call" | custom-call | flops 1073741824 | tf_op jit(solution)/shard_map/pallas_call | solution.py:41
  78.5 2.0 %collective-permute-start.7 = (bf16[528,512]{1,0:T(8,128)(2,1)}, bf16[528,512]{1,0:T(8,128)(2,1)S(1)}, u32[]{:S(2)}, u32[]{:S(2)}) collective-permute-start(bf16[528,512]{1,0:T(8,128)(2,1)} %get-tuple-element.58), channel_id=1, source_target_pairs={{0,8},{8,16},{16,24},{24,0},{1,9},{9,17},{17,25},{25,1},{2,10},{10... | collective-permute-start | bytes 1622024 | tf_op jit(solution)/shard_map/ppermute | solution.py:27
  80.5 2.7 %collective-permute-start.6 = (bf16[528,512]{1,0:T(8,128)(2,1)S(1)}, bf16[528,512]{1,0:T(8,128)(2,1)S(1)}, u32[]{:S(2)}, u32[]{:S(2)}) collective-permute-start(bf16[528,512]{1,0:T(8,128)(2,1)S(1)} %copy-done.7), channel_id=1, source_target_pairs={{0,16},{8,24},{16,0},{24,8},{1,17},{9,25},{17,1},{25,9},{2,18},{10... | collective-permute-start | bytes 1622024 | tf_op jit(solution)/shard_map/ppermute | solution.py:27
  83.2 2.6 %shard_map.128 = (bf16[528,512]{1,0:T(8,128)(2,1)}, bf16[528,512]{1,0:T(8,128)(2,1)}) custom-call(s32[8]{0:T(128)S(1)} %stack.56.chunks, bf16[2048,1024]{1,0:T(8,128)(2,1)S(1)} %copy-done, bf16[1024,1024]{1,0:T(8,128)(2,1)S(1)} %shard_map.126.grad_pre, bf16[64,256]{1,0:T(8,128)(2,1)S(1)} %get-tuple-element.47.piece, bf16[528,512]{1,0:T(8,128)(2,1)} %get-tuple-element.48.after), custom_call_target="tpu_custom_call" | custom-call | flops 1073741824 | tf_op jit(solution)/shard_map/pallas_call | solution.py:41
  88.8 2.7 %collective-permute-start = (bf16[528,512]{1,0:T(8,128)(2,1)S(1)}, bf16[528,512]{1,0:T(8,128)(2,1)S(1)}, u32[]{:S(2)}, u32[]{:S(2)}) collective-permute-start(bf16[528,512]{1,0:T(8,128)(2,1)S(1)} %copy-done.6), channel_id=1, source_target_pairs={{0,64},{32,96},{64,0},{96,32},{1,65},{33,97},{65,1},{97,33},{2,66}... | collective-permute-start | bytes 1622024 | tf_op jit(solution)/shard_map/ppermute | solution.py:27
  91.5 2.9 %collective-permute-done.7.up = bf16[528,512]{1,0:T(8,128)(2,1)S(1)} collective-permute-done((bf16[528,512]{1,0:T(8,128)(2,1)}, bf16[528,512]{1,0:T(8,128)(2,1)S(1)}, u32[]{:S(2)}, u32[]{:S(2)}) %collective-permute-start.7) | collective-permute-done | bytes 540704 | tf_op jit(solution)/shard_map/ppermute | solution.py:27
  94.3 3.0 %collective-permute-start.2 = (bf16[528,512]{1,0:T(8,128)(2,1)}, bf16[528,512]{1,0:T(8,128)(2,1)S(1)}, u32[]{:S(2)}, u32[]{:S(2)}) collective-permute-start(bf16[528,512]{1,0:T(8,128)(2,1)} %get-tuple-element.49.after), channel_id=1, source_target_pairs={{0,96},{32,0},{64,32},{96,64},{1,97},{33,1},{65,33},{97,65},{2,98}... | collective-permute-start | bytes 1622024 | tf_op jit(solution)/shard_map/ppermute | solution.py:27
  99.2 7.1 %collective-permute-done.6.far = bf16[528,512]{1,0:T(8,128)(2,1)S(1)} collective-permute-done((bf16[528,512]{1,0:T(8,128)(2,1)S(1)}, bf16[528,512]{1,0:T(8,128)(2,1)S(1)}, u32[]{:S(2)}, u32[]{:S(2)}) %collective-permute-start.6) | collective-permute-done | bytes 540704 | tf_op jit(solution)/shard_map/ppermute | solution.py:27
  112.3 3.9 %collective-permute-done.far = bf16[528,512]{1,0:T(8,128)(2,1)S(1)} collective-permute-done((bf16[528,512]{1,0:T(8,128)(2,1)S(1)}, bf16[528,512]{1,0:T(8,128)(2,1)S(1)}, u32[]{:S(2)}, u32[]{:S(2)}) %collective-permute-start) | collective-permute-done | bytes 540704 | tf_op jit(solution)/shard_map/ppermute | solution.py:27
  117.1 3.2 %collective-permute-start.5 = (bf16[192,512]{1,0:T(8,128)(2,1)S(1)}, bf16[192,512]{1,0:T(8,128)(2,1)S(1)}, u32[]{:S(2)}, u32[]{:S(2)}) collective-permute-start(bf16[192,512]{1,0:T(8,128)(2,1)S(1)} %get-tuple-element.55), channel_id=1, source_target_pairs={{0,24},{8,0},{16,8},{24,16},{1,25},{9,1},{17,9},{25,17},{2,26},{10... | collective-permute-start | bytes 589832 | tf_op jit(solution)/shard_map/ppermute | solution.py:27
  122.0 6.1 %collective-permute-done.4.a1 = bf16[192,512]{1,0:T(8,128)(2,1)S(1)} collective-permute-done((bf16[192,512]{1,0:T(8,128)(2,1)S(1)}, bf16[192,512]{1,0:T(8,128)(2,1)S(1)}, u32[]{:S(2)}, u32[]{:S(2)}) %collective-permute-start.4) | collective-permute-done | bytes 196640 | tf_op jit(solution)/shard_map/ppermute | solution.py:27
  (45 shorter events, 16.2 us)
Async XLA Ops:
  0.6 20.9 %copy-start.8 = (f32[8]{0:T(128)S(1)}, f32[8]{0:T(128)}, u32[]{:S(2)}) copy-start(f32[8]{0:T(128)} %param.14) | copy-start | bytes 100
  0.6 21.0 %copy-start.3 = (bf16[1024,256]{1,0:T(8,128)(2,1)S(1)}, bf16[1024,256]{1,0:T(8,128)(2,1)}, u32[]{:S(2)}) copy-start(bf16[1024,256]{1,0:T(8,128)(2,1)} %w_out.1) | copy-start | bytes 1572868
  13.4 16.0 %copy-start.1 = (f32[1024]{0:T(1024)S(1)}, f32[1024]{0:T(1024)}, u32[]{:S(2)}) copy-start(f32[1024]{0:T(1024)} %param.10) | copy-start | bytes 12292
  13.5 16.0 %copy-start.2 = (f32[1024]{0:T(1024)S(1)}, f32[1024]{0:T(1024)}, u32[]{:S(2)}) copy-start(f32[1024]{0:T(1024)} %param.11) | copy-start | bytes 12292
  13.5 16.0 %all-to-all-start = ((f32[16,2,1024]{2,1,0:T(2,128)}), f32[16,2,1024]{2,1,0:T(2,128)S(1)}, u32[]{:S(2)}, u32[]{:S(2)}) async-start(f32[16,2,1024]{2,1,0:T(2,128)} %get-tuple-element.37.after), calls=%async_computation | async-start | bytes 262144 | tf_op jit(solution)/shard_map/all_to_all | solution.py:31
  27.2 10.4 %copy-start.5 = (s32[1024]{0:T(1024)S(1)}, s32[1024]{0:T(1024)}, u32[]{:S(2)}) copy-start(s32[1024]{0:T(1024)} %param.15) | copy-start | bytes 12292
  33.2 9.9 %all-to-all-start.1 = ((f32[8,8,128]{2,1,0:T(8,128)}), f32[8,8,128]{2,1,0:T(8,128)S(1)}, u32[]{:S(2)}, u32[]{:S(2)}) async-start(f32[8,8,128]{2,1,0:T(8,128)} %get-tuple-element.40.after), calls=%async_computation.1 | async-start | bytes 65536 | tf_op jit(solution)/shard_map/all_to_all | solution.py:31
  47.8 19.7 %all-to-all-start.2 = ((bf16[16,88,256]{2,1,0:T(8,128)(2,1)}), bf16[16,88,256]{2,1,0:T(8,128)(2,1)S(1)}, u32[]{:S(2)}, u32[]{:S(2)}) async-start(bf16[16,88,256]{2,1,0:T(8,128)(2,1)} %get-tuple-element.45), calls=%async_computation.2 | async-start | bytes 1441792 | tf_op jit(solution)/shard_map/all_to_all | solution.py:31
  71.2 4.7 %copy-start = (bf16[2048,1024]{1,0:T(8,128)(2,1)S(1)}, bf16[2048,1024]{1,0:T(8,128)(2,1)}, u32[]{:S(2)}) copy-start(bf16[2048,1024]{1,0:T(8,128)(2,1)} %shard_map.122.turned_hbm.turned) | copy-start | bytes 12582916
  75.8 4.7 %copy-start.7 = (bf16[528,512]{1,0:T(8,128)(2,1)S(1)}, bf16[528,512]{1,0:T(8,128)(2,1)}, u32[]{:S(2)}) copy-start(bf16[528,512]{1,0:T(8,128)(2,1)} %get-tuple-element.57) | copy-start | bytes 1622020
  78.5 8.9 %copy-start.4 = (bf16[528,512]{1,0:T(8,128)(2,1)S(1)}, bf16[528,512]{1,0:T(8,128)(2,1)}, u32[]{:S(2)}) copy-start(bf16[528,512]{1,0:T(8,128)(2,1)} %get-tuple-element.48.after) | copy-start | bytes 1622020
  78.5 10.3 %copy-start.6 = (bf16[528,512]{1,0:T(8,128)(2,1)S(1)}, bf16[528,512]{1,0:T(8,128)(2,1)}, u32[]{:S(2)}) copy-start(bf16[528,512]{1,0:T(8,128)(2,1)} %get-tuple-element.51) | copy-start | bytes 1622020
  78.5 15.8 %collective-permute-start.7 = (bf16[528,512]{1,0:T(8,128)(2,1)}, bf16[528,512]{1,0:T(8,128)(2,1)S(1)}, u32[]{:S(2)}, u32[]{:S(2)}) collective-permute-start(bf16[528,512]{1,0:T(8,128)(2,1)} %get-tuple-element.58), channel_id=1, source_target_pairs={{0,8},{8,16},{16,24},{24,0},{1,9},{9,17},{17,25},{25,1},{2,10},{10... | collective-permute-start | bytes 1622024 | tf_op jit(solution)/shard_map/ppermute | solution.py:27
  80.5 25.8 %collective-permute-start.6 = (bf16[528,512]{1,0:T(8,128)(2,1)S(1)}, bf16[528,512]{1,0:T(8,128)(2,1)S(1)}, u32[]{:S(2)}, u32[]{:S(2)}) collective-permute-start(bf16[528,512]{1,0:T(8,128)(2,1)S(1)} %copy-done.7), channel_id=1, source_target_pairs={{0,16},{8,24},{16,0},{24,8},{1,17},{9,25},{17,1},{25,9},{2,18},{10... | collective-permute-start | bytes 1622024 | tf_op jit(solution)/shard_map/ppermute | solution.py:27
  85.8 20.5 %collective-permute-start.8 = (bf16[528,512]{1,0:T(8,128)(2,1)}, bf16[528,512]{1,0:T(8,128)(2,1)S(1)}, u32[]{:S(2)}, u32[]{:S(2)}) collective-permute-start(bf16[528,512]{1,0:T(8,128)(2,1)} %get-tuple-element.59), channel_id=1, source_target_pairs={{0,24},{8,0},{16,8},{24,16},{1,25},{9,1},{17,9},{25,17},{2,26},{10... | collective-permute-start | bytes 1622024 | tf_op jit(solution)/shard_map/ppermute | solution.py:27
  87.3 23.2 %collective-permute-start.1 = (bf16[528,512]{1,0:T(8,128)(2,1)S(1)}, bf16[528,512]{1,0:T(8,128)(2,1)S(1)}, u32[]{:S(2)}, u32[]{:S(2)}) collective-permute-start(bf16[528,512]{1,0:T(8,128)(2,1)S(1)} %copy-done.4), channel_id=1, source_target_pairs={{0,32},{32,64},{64,96},{96,0},{1,33},{33,65},{65,97},{97,1},{2,34}... | collective-permute-start | bytes 1622024 | tf_op jit(solution)/shard_map/ppermute | solution.py:27
  88.8 27.4 %collective-permute-start = (bf16[528,512]{1,0:T(8,128)(2,1)S(1)}, bf16[528,512]{1,0:T(8,128)(2,1)S(1)}, u32[]{:S(2)}, u32[]{:S(2)}) collective-permute-start(bf16[528,512]{1,0:T(8,128)(2,1)S(1)} %copy-done.6), channel_id=1, source_target_pairs={{0,64},{32,96},{64,0},{96,32},{1,65},{33,97},{65,1},{97,33},{2,66}... | collective-permute-start | bytes 1622024 | tf_op jit(solution)/shard_map/ppermute | solution.py:27
  94.3 21.9 %collective-permute-start.2 = (bf16[528,512]{1,0:T(8,128)(2,1)}, bf16[528,512]{1,0:T(8,128)(2,1)S(1)}, u32[]{:S(2)}, u32[]{:S(2)}) collective-permute-start(bf16[528,512]{1,0:T(8,128)(2,1)} %get-tuple-element.49.after), channel_id=1, source_target_pairs={{0,96},{32,0},{64,32},{96,64},{1,97},{33,1},{65,33},{97,65},{2,98}... | collective-permute-start | bytes 1622024 | tf_op jit(solution)/shard_map/ppermute | solution.py:27
  107.1 13.2 %collective-permute-start.10 = (bf16[192,512]{1,0:T(8,128)(2,1)S(1)}, bf16[192,512]{1,0:T(8,128)(2,1)S(1)}, u32[]{:S(2)}, u32[]{:S(2)}) collective-permute-start(bf16[192,512]{1,0:T(8,128)(2,1)S(1)} %get-tuple-element.62), channel_id=1, source_target_pairs={{0,32},{32,64},{64,96},{96,0},{1,33},{33,65},{65,97},{97,1},{2,34}... | collective-permute-start | bytes 589832 | tf_op jit(solution)/shard_map/ppermute | solution.py:27
  108.8 11.6 %collective-permute-start.11 = (bf16[192,512]{1,0:T(8,128)(2,1)S(1)}, bf16[192,512]{1,0:T(8,128)(2,1)S(1)}, u32[]{:S(2)}, u32[]{:S(2)}) collective-permute-start(bf16[192,512]{1,0:T(8,128)(2,1)S(1)} %get-tuple-element.63), channel_id=1, source_target_pairs={{0,96},{32,0},{64,32},{96,64},{1,97},{33,1},{65,33},{97,65},{2,98}... | collective-permute-start | bytes 589832 | tf_op jit(solution)/shard_map/ppermute | solution.py:27
  110.5 11.5 %collective-permute-start.9 = (bf16[192,512]{1,0:T(8,128)(2,1)S(1)}, bf16[192,512]{1,0:T(8,128)(2,1)S(1)}, u32[]{:S(2)}, u32[]{:S(2)}) collective-permute-start(bf16[192,512]{1,0:T(8,128)(2,1)S(1)} %get-tuple-element.61.b0), channel_id=1, source_target_pairs={{0,64},{32,96},{64,0},{96,32},{1,65},{33,97},{65,1},{97,33},{2,66}... | collective-permute-start | bytes 589832 | tf_op jit(solution)/shard_map/ppermute | solution.py:27
  117.0 11.2 %collective-permute-start.4 = (bf16[192,512]{1,0:T(8,128)(2,1)S(1)}, bf16[192,512]{1,0:T(8,128)(2,1)S(1)}, u32[]{:S(2)}, u32[]{:S(2)}) collective-permute-start(bf16[192,512]{1,0:T(8,128)(2,1)S(1)} %get-tuple-element.54), channel_id=1, source_target_pairs={{0,8},{8,16},{16,24},{24,0},{1,9},{9,17},{17,25},{25,1},{2,10},{10... | collective-permute-start | bytes 589832 | tf_op jit(solution)/shard_map/ppermute | solution.py:27
  117.1 11.1 %collective-permute-start.5 = (bf16[192,512]{1,0:T(8,128)(2,1)S(1)}, bf16[192,512]{1,0:T(8,128)(2,1)S(1)}, u32[]{:S(2)}, u32[]{:S(2)}) collective-permute-start(bf16[192,512]{1,0:T(8,128)(2,1)S(1)} %get-tuple-element.55), channel_id=1, source_target_pairs={{0,24},{8,0},{16,8},{24,16},{1,25},{9,1},{17,9},{25,17},{2,26},{10... | collective-permute-start | bytes 589832 | tf_op jit(solution)/shard_map/ppermute | solution.py:27
  120.3 7.9 %collective-permute-start.3 = (bf16[192,512]{1,0:T(8,128)(2,1)S(1)}, bf16[192,512]{1,0:T(8,128)(2,1)S(1)}, u32[]{:S(2)}, u32[]{:S(2)}) collective-permute-start(bf16[192,512]{1,0:T(8,128)(2,1)S(1)} %get-tuple-element.53.a0), channel_id=1, source_target_pairs={{0,16},{8,24},{16,0},{24,8},{1,17},{9,25},{17,1},{25,9},{2,18},{10... | collective-permute-start | bytes 589832 | tf_op jit(solution)/shard_map/ppermute | solution.py:27
where the time goes:
time: 131 us; the launch traced here: 130 us
  Pallas kernels  59.5 us (45%)
  starting transfers between devices  39.2 us (30%)
  waiting for transfers between devices  29.3 us (22%)
    pallas_call x14, Pallas kernels, call(): pl.pallas_call(body, out_shape=shapes, in_specs=[pl.BlockSpec(memory_spac...  59.5 us
    ppermute x12, waiting for transfers between devices, hop(): lax.ppermute(value, axis, [(i, (i + step) % count) for i in range(count)])  21.7 us
    ppermute x12, starting transfers between devices, hop(): lax.ppermute(value, axis, [(i, (i + step) % count) for i in range(count)])  21.7 us
    all_to_all x3, starting transfers between devices, exchange(): return lax.all_to_all(blocks, axes, 0, 0, tiled=True)  17.5 us
    all_to_all x3, waiting for transfers between devices, exchange(): return lax.all_to_all(blocks, axes, 0, 0, tiled=True)  7.57 us
  transfers between devices with their start and end apart: 15, of which 7 were waited for; matrix products, arithmetic and copies ran while one was open for 0% of the time, Pallas kernels for 20%

commit v1 on v0

--- a/solution.py
+++ b/solution.py
@@ -66,8 +66,8 @@
     return (codes.astype(F32) * (2.0 / (buckets - 1.0)) - 1.0).astype(BF16)
 
 
-def decode_body(codes_hbm, w_hbm, hidden_hbm, slope_hbm, sums, codes, weights, hidden, slope, inputs, pre_a, pre_b, totals,
-                code_sem, w_sem, out_sem):
+def decode_body(codes_hbm, w_hbm, hidden_hbm, slope_hbm, sums, base, codes, weights, hidden, slope, inputs, pre_a, pre_b, kept,
+                totals, code_sem, w_sem, out_sem):
     rows, units = hidden.shape
     block, tile = pre_a.shape
     blocks, tiles = rows // block, units // tile
@@ -113,10 +113,18 @@
                 inverse = 1.0 / (both + 2.0)
                 tangent = both * inverse
                 value = x * tangent
-                hidden[at, cols] = value
+                if i == 0:
+                    kept[at, cols] = value
+                else:
+                    hidden[at, cols] = (value - base[:, cols]).astype(BF16)
                 slope[at, cols] = (tangent + (x * (4.0 * inverse)) * ((grown + grown * grown) * inverse)).astype(BF16)
                 first = first + value.reshape(part // 8, 8, strip).sum(0)
                 second = second + (value * value).reshape(part // 8, 8, strip).sum(0)
+            if i == 0:
+                base[:, cols] = jnp.sum(first, 0, keepdims=True) * (1.0 / block)
+                for r in range(block // part):
+                    at = slice(r * part, (r + 1) * part)
+                    hidden[at, cols] = (kept[at, cols] - base[:, cols]).astype(BF16)
             totals[0:8, cols] += first
             totals[8:16, cols] += second
 
@@ -224,7 +232,7 @@
         put(g).wait()
 
 
-def logit_body(total_rows, arrived, gain, bias, hidden_hbm, spread_hbm, coef, parts, hidden, spread, sem):
+def logit_body(total_rows, arrived, gain, bias, base, hidden_hbm, spread_hbm, coef, parts, hidden, spread, sem):
     rows, units = hidden.shape
     block = LANES
     blocks = rows // block
@@ -238,7 +246,7 @@
     inv = lax.rsqrt(var + epsilon)
     coef[0:1, :] = gain[...] * inv
     coef[1:2, :] = bias[...]
-    coef[2:3, :] = mean
+    coef[2:3, :] = mean - base[...]
     coef[3:4, :] = inv
 
     def step(i, carry):
@@ -248,7 +256,7 @@
         total = jnp.zeros((block, LANES), F32)
         for n in range(units // LANES):
             cols = slice(n * LANES, (n + 1) * LANES)
-            value = (hidden[at, cols] - coef[2:3, cols]) * coef[0:1, cols] + coef[1:2, cols]
+            value = (hidden[at, cols].astype(F32) - coef[2:3, cols]) * coef[0:1, cols] + coef[1:2, cols]
             total = total + value * spread[at, cols].astype(F32)
         line = jnp.sum(total.T, 0, keepdims=True)
         for k in range(parts.shape[0]):
@@ -296,7 +304,7 @@
         for n in range(units // LANES):
             cols = slice(n * LANES, (n + 1) * LANES)
             part = weight * spread[at, cols].astype(F32)
-            centred = hidden[at, cols] - coef[2:3, cols]
+            centred = hidden[at, cols].astype(F32) - coef[2:3, cols]
             normed[at, cols] = (centred * coef[0:1, cols] + coef[1:2, cols]).astype(BF16)
             product = part * centred
             totals[0:8, cols] += part.reshape(block // 8, 8, LANES).sum(0)
@@ -320,18 +328,23 @@
             packed[n * (512 // share) + k, 0:share, :] = out[k * share : (k + 1) * share, :]
 
 
+def lefts(turned_hbm, left, sem, z_chunk, x_chunk):
+    quarter = left.shape[1]
+    sub = quarter // 4
+    copies = [pltpu.make_async_copy(turned_hbm.at[span(z_chunk, quarter), :], left.at[0], sem.at[0])]
+    for q in range(4):
+        at = pl.ds(pl.multiple_of(q * quarter + x_chunk * sub, sub), sub)
+        copies.append(pltpu.make_async_copy(turned_hbm.at[at, :], left.at[1, q * sub : (q + 1) * sub, :], sem.at[1 + q]))
+    return copies
+
+
 def ahead_body(chunks, grads, hidden_hbm, spread_hbm, slope_hbm, coef, turned_hbm, terms_hbm, hidden, spread, slope, plain,
                flat, tilted, left, terms, sem, left_sem, out_sem):
     rows, units = hidden.shape
     block = LANES
     blocks = rows // block
-    quarter = left.shape[1]
-    sub = quarter // 4
     wide = units // 2
-    far = [pltpu.make_async_copy(turned_hbm.at[span(chunks[2], quarter), :], left.at[0], left_sem.at[0])]
-    for q in range(4):
-        at = pl.ds(pl.multiple_of(q * quarter + chunks[6] * sub, sub), sub)
-        far.append(pltpu.make_async_copy(turned_hbm.at[at, :], left.at[1, q * sub : (q + 1) * sub, :], left_sem.at[1 + q]))
+    far = lefts(turned_hbm, left, left_sem, chunks[2], chunks[6])
     for i in range(blocks):
         rows_in(hidden_hbm, hidden, sem, 0, i, block).start()
         rows_in(spread_hbm, spread, sem, 1, i, block).start()
@@ -350,7 +363,7 @@
             factor = coef[0:1, cols] * slope[at, cols].astype(F32)
             flat[at, cols] = factor.astype(BF16)
             plain[at, cols] = (factor * (weight * spread[at, cols].astype(F32))).astype(BF16)
-            tilted[at, cols] = (factor * (hidden[at, cols] - coef[2:3, cols])).astype(BF16)
+            tilted[at, cols] = (factor * (hidden[at, cols].astype(F32) - coef[2:3, cols])).astype(BF16)
         return carry
 
     lax.fori_loop(0, blocks, step, 0)
@@ -369,18 +382,24 @@
         put(k).wait()
 
 
-def far_body(total_rows, arrived, coef, terms_hbm, z_hbm, x_hbm, both, grad_gain, grad_bias, loss, piece, terms, held, sem,
-             out_sem):
+def lay_piece(message, piece, below):
+    half = piece.shape[0] // 2
+    wide = piece.shape[1]
+    for n in range(2):
+        message[below:, n * wide : (n + 1) * wide] = piece[n * half : (n + 1) * half, :]
+
+
+def far_body(total_rows, arrived, coef, terms_hbm, z_hbm, x_hbm, both, piece, terms, held_z, held_x, sem, out_sem):
     units = coef.shape[1]
     share, emb = piece.shape
     quarter, wide = terms.shape[1:]
-    some = held.shape[1] - quarter
+    held = (held_z, held_x)
 
     def get(k):
         return pltpu.make_async_copy(terms_hbm.at[k], terms.at[k], sem.at[k])
 
     def put(axis):
-        return pltpu.make_async_copy(held.at[axis], (z_hbm, x_hbm)[axis], out_sem.at[axis])
+        return pltpu.make_async_copy(held[axis], (z_hbm, x_hbm)[axis], out_sem.at[axis])
 
     for k in range(6):
         get(k).start()
@@ -392,16 +411,15 @@
     lines = stat(1) + stat(0)
     for q in range(count):
         cols = slice(q * emb, (q + 1) * emb)
-        grad_bias[:, cols] = lines[q : q + 1]
-        grad_gain[:, cols] = lines[count + q : count + q + 1]
+        both[2:3, cols] = lines[q : q + 1]
+        both[3:4, cols] = lines[count + q : count + q + 1]
         both[0:1, cols] = lines[q : q + 1] / total_rows
         both[1:2, cols] = lines[count + q : count + q + 1] * coef[3:4, cols] / total_rows
-    loss[...] = jnp.sum(stat(2), 0, keepdims=True)[:, 0:LANES] / total_rows
+    both[4:5, 0:emb] = jnp.sum(stat(2), 0, keepdims=True) / total_rows
     piece[...] = jnp.sum(arrived[:, 0:share, :].astype(F32), 0).astype(BF16)
     for axis in range(2):
-        first = axis * 2 * some
-        for n in range(2):
-            held[axis, quarter:, n * 256 : (n + 1) * 256] = piece[first + n * some : first + (n + 1) * some, :]
+        if axis == 1:
+            lay_piece(held_x, piece, quarter)
         for k in range(3):
             get(3 * axis + k).wait()
         for r in range(quarter // LANES):
@@ -411,20 +429,47 @@
                 here = slice(axis * wide + n * LANES, axis * wide + (n + 1) * LANES)
                 value = terms[3 * axis, at, cols].astype(F32) - terms[3 * axis + 1, at, cols].astype(F32) * both[0:1, here]
                 value = value - terms[3 * axis + 2, at, cols].astype(F32) * both[1:2, here]
-                held[axis, at, cols] = value.astype(BF16)
+                held[axis][at, cols] = value.astype(BF16)
         put(axis).start()
     for axis in range(2):
         put(axis).wait()
 
 
-def back_body(grads, hidden_hbm, spread_hbm, slope_hbm, coef, both, grad_pre, hidden, spread, slope, sem):
+def product(axis, chunk, turned, grad_pre, piece, lines, out):
+    rows, wide = lines.shape[0], out.shape[1]
+    sub = rows // 4
+    if axis == 0:
+        left = turned[span(chunk, rows), :]
+    else:
+        for q in range(4):
+            at = pl.ds(pl.multiple_of(q * rows + chunk * sub, sub), sub)
+            lines[q * sub : (q + 1) * sub, :] = turned[at, :]
+        left = lines[...]
+        lay_piece(out, piece, rows)
+    out[0:rows, :] = dot(left, grad_pre[:, axis * wide : (axis + 1) * wide]).astype(BF16)
+
+
+def near_body(chunks, grads, hidden_hbm, spread_hbm, slope_hbm, coef, both, turned_hbm, piece, grad_pre, grad_gain, grad_bias,
+              loss, z1_hbm, x1_hbm, z3_hbm, x3_hbm, hidden, spread, slope, turned, lines, z1, x1, z3, x3, sem,
+              turned_sem, out_sem):
     rows, units = hidden.shape
     block = LANES
     blocks = rows // block
+    parts = turned_sem.shape[0]
+
+    def turn_in(i):
+        at = span(i, turned.shape[0] // parts)
+        return pltpu.make_async_copy(turned_hbm.at[at, :], turned.at[at, :], turned_sem.at[i])
+
     for i in range(blocks):
         rows_in(hidden_hbm, hidden, sem, 0, i, block).start()
         rows_in(spread_hbm, spread, sem, 1, i, block).start()
         rows_in(slope_hbm, slope, sem, 2, i, block).start()
+    for i in range(parts):
+        turn_in(i).start()
+    grad_bias[...] = both[2:3, :]
+    grad_gain[...] = both[3:4, :]
+    loss[...] = both[4:5, 0:LANES]
 
     def step(i, carry):
         at = span(i, block)
@@ -435,45 +480,36 @@
         for n in range(units // LANES):
             cols = slice(n * LANES, (n + 1) * LANES)
             inner = weight * spread[at, cols].astype(F32) - both[0:1, cols]
-            inner = inner - (hidden[at, cols] - coef[2:3, cols]) * both[1:2, cols]
+            inner = inner - (hidden[at, cols].astype(F32) - coef[2:3, cols]) * both[1:2, cols]
             grad_pre[at, cols] = (inner * coef[0:1, cols] * slope[at, cols].astype(F32)).astype(BF16)
         return carry
 
     lax.fori_loop(0, blocks, step, 0)
-
-
-def product_body(jobs, keep, chunks, turned, grad_pre, piece, after, *refs):
+    for i in range(parts):
+        turn_in(i).wait()
+    jobs = ((0, 1, z1, z1_hbm), (1, 1, x1, x1_hbm), (0, 3, z3, z3_hbm), (1, 3, x3, x3_hbm))
+
+    def put(k):
+        return pltpu.make_async_copy(jobs[k][2], jobs[k][3], out_sem.at[k])
+
+    for k, (axis, step_on, held, _) in enumerate(jobs):
+        product(axis, chunks[4 * axis + step_on], turned, grad_pre, piece, lines, held)
+        put(k).start()
+    for k in range(len(jobs)):
+        put(k).wait()
+
+
+def own_body(chunks, turned_hbm, grad_pre, piece, after, z0, x0, left, sem):
     del after
-    count = len(jobs)
-    outs, (lines, held, sem) = refs[:count], refs[count:]
-    rows = lines.shape[0]
-    wide = held.shape[2]
-    some = held.shape[1] - rows
-    sub = rows // 4
-
-    def put(k):
-        return pltpu.make_async_copy(held.at[k], outs[k], sem.at[k])
-
-    for k, (axis, place) in enumerate(jobs):
-        c = chunks[place]
-        out = outs[k] if keep else held.at[k]
-        if axis == "z":
-            left = turned[span(c, rows), :]
-            base, first = 0, 0
-        else:
-            for q in range(4):
-                at = pl.ds(pl.multiple_of(q * rows + c * sub, sub), sub)
-                lines[q * sub : (q + 1) * sub, :] = turned[at, :]
-            left = lines[...]
-            base, first = wide, 2 * some
-        out[0:rows, :] = dot(left, grad_pre[:, base : base + wide]).astype(BF16)
-        for n in range(2):
-            out[rows:, n * 256 : (n + 1) * 256] = piece[first + n * some : first + (n + 1) * some, :]
-        if not keep:
-            put(k).start()
-    if not keep:
-        for k in range(count):
-            put(k).wait()
+    copies = lefts(turned_hbm, left, sem, chunks[0], chunks[4])
+    for copy in copies:
+        copy.start()
+    rows, wide = z0.shape
+    lay_piece(x0, piece, rows)
+    for copy in copies:
+        copy.wait()
+    for axis, out in ((0, z0), (1, x0)):
+        out[0:rows, :] = dot(left[axis], grad_pre[:, axis * wide : (axis + 1) * wide]).astype(BF16)
 
 
 def middle_body(chunk, own, far, up, down, own_out, far_out, up_out, down_out):
@@ -485,26 +521,24 @@
         at = span(lax.rem(me + step, 4), rows)
         total = (own[at, :].astype(F32) + far[at, :].astype(F32)) + (up[at, :].astype(F32) + down[at, :].astype(F32))
         out[0:rows, :] = total.astype(out.dtype)
-        if step:
+        if step and some:
             for back, came in ((0, own), (2, far), (1, up), (3, down)):
                 to = pl.ds(pl.multiple_of(rows + lax.rem(was + 4 - back, 4) * some, some), some)
                 out[to, :] = came[full:, :]
 
 
-def last_body(place, own_a, a0, a2, a1, a3, own_b, b0, b2, b1, b3, hash_hbm, out_hbm, grad_hash, grad_out, sem):
+def last_body(place, own_a, a2, a1, a3, own_b, b0, b2, b1, b3, hash_hbm, out_hbm, grad_hash, grad_out, sem):
     rows, half = own_a.shape
-    some = (a0.shape[0] - rows) // 4
-    share = 4 * some
-    for kind, pieces in ((0, (a0, a2, a1, a3)), (1, (b0, b2, b1, b3))):
-        me = place[1 - kind]
-        for back, came in zip((0, 2, 1, 3), pieces):
-            there = lax.rem(me + 4 - back, 4)
-            for k in range(4):
-                owner = k * 4 + there if kind == 0 else there * 4 + k
-                for n in range(2):
-                    to = pl.ds(pl.multiple_of(owner * share + (2 * kind + n) * some, some), some)
-                    at = slice(rows + k * some, rows + (k + 1) * some)
-                    grad_out[to, :] = came[at, n * 256 : (n + 1) * 256].astype(F32)
+    some = (b0.shape[0] - rows) // 4
+    share = 2 * some
+    emb = grad_out.shape[1]
+    for back, came in zip((0, 2, 1, 3), (b0, b2, b1, b3)):
+        there = lax.rem(place[0] + 4 - back, 4)
+        for k in range(4):
+            for n in range(2):
+                to = pl.ds(pl.multiple_of((there * 4 + k) * share + n * some, some), some)
+                at = slice(rows + k * some, rows + (k + 1) * some)
+                grad_out[to, :] = came[at, n * emb : (n + 1) * emb].astype(F32)
     put_out = pltpu.make_async_copy(grad_out, out_hbm, sem.at[0])
     put_out.start()
     for base, own, came in ((0, own_a, (a2, a1, a3)), (half, own_b, (b2, b1, b3))):
@@ -529,18 +563,19 @@
     share = units // dp
     some = share // 4
     dma = pltpu.SemaphoreType.DMA
-    hidden, slope, sums = call(
+    hidden, slope, sums, base = call(
         decode_body,
         [(hash_codes, "h"), (w_hash, "h")],
-        [((rows, units), F32, "h"), ((rows, units), BF16, "h"), ((dp, 2, units), F32, "v")],
+        [((rows, units), BF16, "h"), ((rows, units), BF16, "h"), ((dp, 2, units), F32, "v"), ((1, units), F32, "v")],
         [
             pltpu.VMEM((rows, codes), jnp.int32),
             pltpu.VMEM((codes, units), BF16),
-            pltpu.VMEM((rows, units), F32),
+            pltpu.VMEM((rows, units), BF16),
             pltpu.VMEM((rows, units), BF16),
             pltpu.VMEM((rows, codes), BF16),
             pltpu.VMEM((256, units // 2), F32),
             pltpu.VMEM((256, units // 2), F32),
+            pltpu.VMEM((256, units), F32),
             pltpu.VMEM((16, units), F32),
             dma((rows // 256,)),
             dma((2,)),
@@ -571,11 +606,12 @@
             (arrived, "v"),
             (norm_gain.reshape(1, units), "v"),
             (norm_bias.reshape(1, units), "v"),
+            (base, "v"),
             (hidden, "h"),
             (spread, "h"),
         ],
         [((8, units), F32, "v"), ((mp, lines, LANES), F32, "v")],
-        [pltpu.VMEM((rows, units), F32), pltpu.VMEM((rows, units), BF16), dma((2, lines))],
+        [pltpu.VMEM((rows, units), BF16), pltpu.VMEM((rows, units), BF16), dma((2, lines))],
         limit=20,
         flops=4 * rows * units,
     )
@@ -594,7 +630,7 @@
         [(logits, "v"), (targets, "v"), (hidden, "h"), (spread, "h"), (coef, "v"), (mixed_t, "v")],
         [((lines, LANES), F32, "v"), ((dp, share + 24, emb), BF16, "v")],
         [
-            pltpu.VMEM((rows, units), F32),
+            pltpu.VMEM((rows, units), BF16),
             pltpu.VMEM((rows, units), BF16),
             pltpu.VMEM((rows, units), BF16),
             pltpu.VMEM((emb, rows), BF16),
@@ -607,7 +643,7 @@
     grad_arrived = exchange(packed, DP)
     here = {axis: lax.axis_index(axis).astype(jnp.int32) for axis in DP}
     chunks = jnp.stack([(here[axis] + step) & 3 for axis in DP for step in range(4)])
-    size = (codes // 4 + some, half)
+    sizes = ((codes // 4, half), (codes // 4 + 2 * some, half))
     (terms,) = call(
         ahead_body,
         [
@@ -620,8 +656,7 @@
             (turned, "h"),
         ],
         [((6, codes // 4, half), BF16, "h")],
-        [pltpu.VMEM((rows, units), F32)]
-        + [pltpu.VMEM((rows, units), BF16)] * 5
+        [pltpu.VMEM((rows, units), BF16)] * 6
         + [
             pltpu.VMEM((2, codes // 4, rows), BF16),
             pltpu.VMEM((6, codes // 4, half), BF16),
@@ -632,53 +667,52 @@
         flops=6 * rows * half * codes,
         limit=30,
     )
-    far_z, far_x, both, grad_gain, grad_bias, loss, piece = call(
+    far_z, far_x, both, piece = call(
         functools.partial(far_body, float(total_rows)),
         [(grad_arrived, "v"), (coef, "v"), (terms, "h")],
         [
-            (size, BF16, "h"),
-            (size, BF16, "h"),
+            (sizes[0], BF16, "h"),
+            (sizes[1], BF16, "h"),
             ((8, units), F32, "p"),
-            ((1, units), F32, "v"),
-            ((1, units), F32, "v"),
-            ((1, LANES), F32, "v"),
             ((share, emb), BF16, "p"),
         ],
-        [pltpu.VMEM((6, codes // 4, half), BF16), pltpu.VMEM((2, *size), BF16), dma((6,)), dma((2,))],
+        [pltpu.VMEM((6, codes // 4, half), BF16)] + [pltpu.VMEM(size, BF16) for size in sizes] + [dma((6,)), dma((2,))],
         limit=10,
         flops=8 * rows * units,
     )
-    (grad_pre,) = call(
-        back_body,
-        [(grads, "v"), (hidden, "h"), (spread, "h"), (slope, "h"), (coef, "v"), (both, "p")],
-        [((rows, units), BF16, "p")],
+    near = call(
+        near_body,
         [
-            pltpu.VMEM((rows, units), F32),
-            pltpu.VMEM((rows, units), BF16),
-            pltpu.VMEM((rows, units), BF16),
-            dma((3, lines)),
+            (chunks, "s"),
+            (grads, "v"),
+            (hidden, "h"),
+            (spread, "h"),
+            (slope, "h"),
+            (coef, "v"),
+            (both, "p"),
+            (turned, "h"),
+            (piece, "p"),
         ],
+        [((rows, units), BF16, "p"), ((1, units), F32, "v"), ((1, units), F32, "v"), ((1, LANES), F32, "v")]
+        + [(size, BF16, "h") for size in sizes * 2],
+        [pltpu.VMEM((rows, units), BF16)] * 3
+        + [pltpu.VMEM((codes, rows), BF16), pltpu.VMEM((codes // 4, rows), BF16)]
+        + [pltpu.VMEM(size, BF16) for size in sizes * 2]
+        + [dma((3, lines)), dma((4,)), dma((4,))],
         limit=20,
-        flops=8 * rows * units,
-    )
-
-
-    def products(steps, keep, after):
-        jobs = [(axis, 4 * DP.index(axis) + step) for step in steps for axis in DP]
-        outs = call(
-            functools.partial(product_body, jobs, keep),
-            [(chunks, "s"), (turned, "p"), (grad_pre, "p"), (piece, "p"), (after, "h")],
-            [(size, BF16, "p" if keep else "h")] * len(jobs),
-            [pltpu.VMEM((codes // 4, rows), BF16), pltpu.VMEM((1 if keep else len(jobs), *size), BF16), dma((len(jobs),))],
-            flops=2 * rows * half * (codes // 4) * len(jobs),
-            limit=8,
-        )
-        return {(axis, place & 3): out for (axis, place), out in zip(jobs, outs)}
-
-    made = {("z", 2): far_z, ("x", 2): far_x}
-    made.update(products((1,), False, terms))
-    made.update(products((3,), False, made["z", 1]))
-    made.update(products((0,), True, made["z", 3]))
+        flops=2 * rows * half * codes,
+    )
+    grad_pre, grad_gain, grad_bias, loss = near[:4]
+    own_z, own_x = call(
+        own_body,
+        [(chunks, "s"), (turned, "h"), (grad_pre, "p"), (piece, "p"), (near[7], "h")],
+        [(size, BF16, "p") for size in sizes],
+        [pltpu.VMEM((2, codes // 4, rows), BF16), dma((5,))],
+        limit=6,
+        flops=rows * half * codes,
+    )
+    made = {("z", 2): far_z, ("x", 2): far_x, ("z", 0): own_z, ("x", 0): own_x}
+    made.update(zip((("z", 1), ("x", 1), ("z", 3), ("x", 3)), near[4:]))
     got = {(axis, step): hop(made[axis, step], axis, step) for step in (2, 1, 3) for axis in DP}
     other = {"z": "x", "x": "z"}
     last = []
@@ -687,11 +721,11 @@
             middle_body,
             [(jnp.stack([here[other[axis]], here[axis]]), "s"), (made[axis, 0], "p")]
             + [(got[axis, step], "p") for step in (2, 1, 3)],
-            [((codes // 16, half), F32, "p")] + [((codes // 16 + 4 * some, half), BF16, "p")] * 3,
+            [((codes // 16, half), F32, "p")] + [((codes // 16 + 8 * some * (axis == "x"), half), BF16, "p")] * 3,
             limit=4,
             flops=rows * units,
         )
-        last += [own, far] + [hop(v, other[axis], step) for v, step in ((far, 2), (up, 1), (down, 3))]
+        last += [own] + [far] * (axis == "x") + [hop(v, other[axis], step) for v, step in ((far, 2), (up, 1), (down, 3))]
     grad_hash, grad_out = call(
         last_body,
         [(jnp.stack([here["z"], here["x"]]), "s")] + [(v, "p") for v in last],

time: 131 us -> 129 us (0.985)
    pallas_call x14 -> x12, Pallas kernels: 59.5 us -> 59 us  [call(): pl.pallas_call(body, out_shape=shapes, in_specs=[pl.BlockSpec(memory_spac...]
  transfers between devices with their start and end apart: 15 -> 15, of which waited for: 7 -> 6; matrix products, arithmetic and copies ran while one was open for 0% -> 0% of each run, Pallas kernels for 20% -> 19%
where the time goes in v1:
time: 129 us; the launch traced here: 128 us
  Pallas kernels  59 us (46%)
  starting transfers between devices  38.2 us (30%)
  waiting for transfers between devices  29.7 us (23%)
    pallas_call x12, Pallas kernels, call(): pl.pallas_call(body, out_shape=shapes, in_specs=[pl.BlockSpec(memory_spac...  59 us
    ppermute x12, waiting for transfers between devices, hop(): lax.ppermute(value, axis, [(i, (i + step) % count) for i in range(count)])  22.2 us
    ppermute x12, starting transfers between devices, hop(): lax.ppermute(value, axis, [(i, (i + step) % count) for i in range(count)])  20.7 us
    all_to_all x3, starting transfers between devices, exchange(): return lax.all_to_all(blocks, axes, 0, 0, tiled=True)  17.6 us
    all_to_all x3, waiting for transfers between devices, exchange(): return lax.all_to_all(blocks, axes, 0, 0, tiled=True)  7.52 us
  transfers between devices with their start and end apart: 15, of which 6 were waited for; matrix products, arithmetic and copies ran while one was open for 0% of the time, Pallas kernels for 19%

profile of v1, /device:TPU:0, one launch (start us, length us, event | category | flops | bytes accessed | tf_op | source)
XLA Modules:
  0.0 128.3 jit_solution(17761153517521257299)
XLA Ops:
  0.7 12.9 %shard_map.119 = (bf16[1024,1024]{1,0:T(8,128)(2,1)}, bf16[1024,1024]{1,0:T(8,128)(2,1)}, f32[16,2,1024]{2,1,0:T(2,128)}, f32[1,1024]{1,0:T(1,128)S(1)}) custom-call(s32[1024,2048]{1,0:T(8,128)} %codes_hbm.3, bf16[2048,1024]{1,0:T(8,128)(2,1)} %w_hbm.1), custom_call_target="tpu_custom_call" | custom-call | flops 4294967296 | tf_op jit(solution)/shard_map/pallas_call | solution.py:41
  13.5 8.0 %all-to-all-start = ((f32[16,2,1024]{2,1,0:T(2,128)}), f32[16,2,1024]{2,1,0:T(2,128)S(1)}, u32[]{:S(2)}, u32[]{:S(2)}) async-start(f32[16,2,1024]{2,1,0:T(2,128)} %get-tuple-element.39.after), calls=%async_computation | async-start | bytes 262144 | tf_op jit(solution)/shard_map/all_to_all | solution.py:31
  21.7 5.6 %shard_map.120 = (bf16[1024,1024]{1,0:T(8,128)(2,1)}, f32[256,1024]{1,0:T(8,128)S(1)}) custom-call(f32[16,2,1024]{2,1,0:T(2,128)} %get-tuple-element.39.after, bf16[8192,256]{1,0:T(8,128)(2,1)} %bitcast.21, f32[1,512]{1,0:T(1,128)S(1)} %reshape_tile.3.mix, bf16[1024,256]{1,0:T(8,128)(2,1)S(1)} %copy-done.2), custom_call_target="tpu_custom_call" | custom-call | flops 2147483648 | tf_op jit(solution)/shard_map/pallas_call | solution.py:41
  27.4 2.2 %all-to-all-done.arrived = f32[16,2,1024]{2,1,0:T(2,128)S(1)} async-done(((f32[16,2,1024]{2,1,0:T(2,128)}), f32[16,2,1024]{2,1,0:T(2,128)S(1)}, u32[]{:S(2)}, u32[]{:S(2)}) %all-to-all-start) | async-done | bytes 131104 | tf_op jit(solution)/shard_map/all_to_all | solution.py:31
  29.5 3.4 %shard_map.121 = (f32[8,1024]{1,0:T(8,128)S(1)}, f32[8,8,128]{2,1,0:T(8,128)}) custom-call(f32[16,2,1024]{2,1,0:T(2,128)S(1)} %all-to-all-done.arrived, f32[1,1024]{1,0:T(1,128)S(1)} %bitcast.19, f32[1,1024]{1,0:T(1,128)S(1)} %bitcast.20, f32[1,1024]{1,0:T(1,128)S(1)} %get-tuple-element.40.base, bf16[1024,1024]{1,0:T(8,128)(2,1)} %get-tuple-element.41.hidden_hbm, ...), custom_call_target="tpu_custom_call" | custom-call | flops 4194304 | tf_op jit(solution)/shard_map/pallas_call | solution.py:41
  32.9 4.5 %all-to-all-start.1 = ((f32[8,8,128]{2,1,0:T(8,128)}), f32[8,8,128]{2,1,0:T(8,128)S(1)}, u32[]{:S(2)}, u32[]{:S(2)}) async-start(f32[8,8,128]{2,1,0:T(8,128)} %get-tuple-element.43.after), calls=%async_computation.1 | async-start | bytes 65536 | tf_op jit(solution)/shard_map/all_to_all | solution.py:31
  37.5 5.3 %all-to-all-done.1.arrived = f32[8,8,128]{2,1,0:T(8,128)S(1)} async-done(((f32[8,8,128]{2,1,0:T(8,128)}), f32[8,8,128]{2,1,0:T(8,128)S(1)}, u32[]{:S(2)}, u32[]{:S(2)}) %all-to-all-start.1) | async-done | bytes 32800 | tf_op jit(solution)/shard_map/all_to_all | solution.py:31
  42.9 4.2 %shard_map.123 = (f32[8,128]{1,0:T(8,128)S(1)}, bf16[16,88,256]{2,1,0:T(8,128)(2,1)}) custom-call(f32[8,8,128]{2,1,0:T(8,128)S(1)} %all-to-all-done.1.arrived, f32[8,128]{1,0:T(8,128)S(1)} %convert_bitcast_fusion.labels, bf16[1024,1024]{1,0:T(8,128)(2,1)} %get-tuple-element.41.hidden_hbm, bf16[1024,1024]{1,0:T(8,128)(2,1)} %get-tuple-element.42.spread_hbm, ...), custom_call_target="tpu_custom_call" | custom-call | flops 536870912 | tf_op jit(solution)/shard_map/pallas_call | solution.py:41
  47.1 5.1 %all-to-all-start.2 = ((bf16[16,88,256]{2,1,0:T(8,128)(2,1)}), bf16[16,88,256]{2,1,0:T(8,128)(2,1)S(1)}, u32[]{:S(2)}, u32[]{:S(2)}) async-start(bf16[16,88,256]{2,1,0:T(8,128)(2,1)} %get-tuple-element.48), calls=%async_computation.2 | async-start | bytes 1441792 | tf_op jit(solution)/shard_map/all_to_all | solution.py:31
  52.2 5.5 %shard_map.122.turned_hbm = bf16[2048,1024]{1,0:T(8,128)(2,1)} custom-call(s32[1024,2048]{1,0:T(8,128)} %codes_hbm.3, f32[8,8,128]{2,1,0:T(8,128)} %get-tuple-element.43.after), custom_call_target="tpu_custom_call" | custom-call | flops 4294967296 | tf_op jit(solution)/shard_map/pallas_call | solution.py:41
  57.8 8.6 %shard_map.124.terms_hbm = bf16[6,512,512]{2,1,0:T(8,128)(2,1)} custom-call(s32[8]{0:T(128)S(1)} %stack.56.chunks, f32[8,128]{1,0:T(8,128)S(1)} %get-tuple-element.46.grads, bf16[1024,1024]{1,0:T(8,128)(2,1)} %get-tuple-element.41.hidden_hbm, bf16[1024,1024]{1,0:T(8,128)(2,1)} %get-tuple-element.42.spread_hbm, ...), custom_call_target="tpu_custom_call" | custom-call | flops 6442450944 | tf_op jit(solution)/shard_map/pallas_call | solution.py:41
  66.4 3.0 %shard_map.125 = (bf16[512,512]{1,0:T(8,128)(2,1)}, bf16[544,512]{1,0:T(8,128)(2,1)}, f32[8,1024]{1,0:T(8,128)S(1)}, bf16[64,256]{1,0:T(8,128)(2,1)S(1)}) custom-call(bf16[16,88,256]{2,1,0:T(8,128)(2,1)S(1)} %all-to-all-done.2.arrived, f32[8,1024]{1,0:T(8,128)S(1)} %get-tuple-element.44.coef, bf16[6,512,512]{2,1,0:T(8,128)(2,1)} %shard_map.124.terms_hbm), custom_call_target="tpu_custom_call" | custom-call | flops 8388608 | tf_op jit(solution)/shard_map/pallas_call | solution.py:41
  69.4 8.9 %shard_map.126 = (bf16[1024,1024]{1,0:T(8,128)(2,1)S(1)}, f32[1,1024]{1,0:T(1,128)}, f32[1,1024]{1,0:T(1,128)}, f32[1,128]{1,0:T(1,128)}, bf16[512,512]{1,0:T(8,...) custom-call(s32[8]{0:T(128)S(1)} %stack.56.chunks, ...), custom_call_target="tpu_custom_call" | custom-call | flops 2147483648 | tf_op jit(solution)/shard_map/pallas_call | solution.py:41
  78.3 2.0 %collective-permute-start.1 = (bf16[512,512]{1,0:T(8,128)(2,1)}, bf16[512,512]{1,0:T(8,128)(2,1)S(1)}, u32[]{:S(2)}, u32[]{:S(2)}) collective-permute-start(bf16[512,512]{1,0:T(8,128)(2,1)} %get-tuple-element.55), channel_id=1, source_target_pairs={{0,32},{32,64},{64,96},{96,0},{1,33},{33,65},{65,97},{97,1},{2,34}... | collective-permute-start | bytes 1572872 | tf_op jit(solution)/shard_map/ppermute | solution.py:27
  87.1 6.1 %collective-permute-done.1.up = bf16[512,512]{1,0:T(8,128)(2,1)S(1)} collective-permute-done((bf16[512,512]{1,0:T(8,128)(2,1)}, bf16[512,512]{1,0:T(8,128)(2,1)S(1)}, u32[]{:S(2)}, u32[]{:S(2)}) %collective-permute-start.1) | collective-permute-done | bytes 524320 | tf_op jit(solution)/shard_map/ppermute | solution.py:27
  93.2 1.9 %collective-permute-start = (bf16[512,512]{1,0:T(8,128)(2,1)S(1)}, bf16[512,512]{1,0:T(8,128)(2,1)S(1)}, u32[]{:S(2)}, u32[]{:S(2)}) collective-permute-start(bf16[512,512]{1,0:T(8,128)(2,1)S(1)} %copy-done.5), channel_id=1, source_target_pairs={{0,64},{32,96},{64,0},{96,32},{1,65},{33,97},{65,1},{97,33},{2,66}... | collective-permute-start | bytes 1572872 | tf_op jit(solution)/shard_map/ppermute | solution.py:27
  95.2 3.4 %shard_map.127 = (bf16[512,512]{1,0:T(8,128)(2,1)S(1)}, bf16[544,512]{1,0:T(8,128)(2,1)S(1)}) custom-call(s32[8]{0:T(128)S(1)} %stack.56.chunks, bf16[2048,1024]{1,0:T(8,128)(2,1)} %shard_map.122.turned_hbm, bf16[1024,1024]{1,0:T(8,128)(2,1)S(1)} %get-tuple-element.51.grad_pre, bf16[64,256]{1,0:T(8,128)(2,1)S(1)} %get-tuple-element.50.piece, ...), custom_call_target="tpu_custom_call" | custom-call | flops 1073741824 | tf_op jit(solution)/shard_map/pallas_call | solution.py:41
  98.7 9.5 %collective-permute-done.2.down = bf16[512,512]{1,0:T(8,128)(2,1)S(1)} collective-permute-done((bf16[512,512]{1,0:T(8,128)(2,1)}, bf16[512,512]{1,0:T(8,128)(2,1)S(1)}, u32[]{:S(2)}, u32[]{:S(2)}) %collective-permute-start.2) | collective-permute-done | bytes 524320 | tf_op jit(solution)/shard_map/ppermute | solution.py:27
  108.9 1.9 %collective-permute-start.3 = (bf16[128,512]{1,0:T(8,128)(2,1)S(1)}, bf16[128,512]{1,0:T(8,128)(2,1)S(1)}, u32[]{:S(2)}, u32[]{:S(2)}) collective-permute-start(bf16[128,512]{1,0:T(8,128)(2,1)S(1)} %get-tuple-element.58), channel_id=1, source_target_pairs={{0,16},{8,24},{16,0},{24,8},{1,17},{9,25},{17,1},{25,9},{2,18},{10... | collective-permute-start | bytes 393224 | tf_op jit(solution)/shard_map/ppermute | solution.py:27
  111.7 2.6 %collective-permute-start.10 = (bf16[256,512]{1,0:T(8,128)(2,1)S(1)}, bf16[256,512]{1,0:T(8,128)(2,1)S(1)}, u32[]{:S(2)}, u32[]{:S(2)}) collective-permute-start(bf16[256,512]{1,0:T(8,128)(2,1)S(1)} %get-tuple-element.66), channel_id=1, source_target_pairs={{0,32},{32,64},{64,96},{96,0},{1,33},{33,65},{65,97},{97,1},{2,34}... | collective-permute-start | bytes 786440 | tf_op jit(solution)/shard_map/ppermute | solution.py:27
  117.0 2.8 %collective-permute-start.5 = (bf16[128,512]{1,0:T(8,128)(2,1)S(1)}, bf16[128,512]{1,0:T(8,128)(2,1)S(1)}, u32[]{:S(2)}, u32[]{:S(2)}) collective-permute-start(bf16[128,512]{1,0:T(8,128)(2,1)S(1)} %get-tuple-element.60), channel_id=1, source_target_pairs={{0,24},{8,0},{16,8},{24,16},{1,25},{9,1},{17,9},{25,17},{2,26},{10... | collective-permute-start | bytes 393224 | tf_op jit(solution)/shard_map/ppermute | solution.py:27
  119.8 2.9 %collective-permute-done.4.a1 = bf16[128,512]{1,0:T(8,128)(2,1)S(1)} collective-permute-done((bf16[128,512]{1,0:T(8,128)(2,1)S(1)}, bf16[128,512]{1,0:T(8,128)(2,1)S(1)}, u32[]{:S(2)}, u32[]{:S(2)}) %collective-permute-start.4) | collective-permute-done | bytes 131104 | tf_op jit(solution)/shard_map/ppermute | solution.py:27
  122.7 3.7 %collective-permute-done.9.b2 = bf16[256,512]{1,0:T(8,128)(2,1)S(1)} collective-permute-done((bf16[256,512]{1,0:T(8,128)(2,1)S(1)}, bf16[256,512]{1,0:T(8,128)(2,1)S(1)}, u32[]{:S(2)}, u32[]{:S(2)}) %collective-permute-start.9) | collective-permute-done | bytes 262176 | tf_op jit(solution)/shard_map/ppermute | solution.py:27
  126.4 1.8 %shard_map.130 = (f32[128,1024]{1,0:T(8,128)}, f32[1024,256]{1,0:T(8,128)}) custom-call(s32[2]{0:T(128)S(1)} %pad_add_fusion.chunk.place, f32[128,512]{1,0:T(8,128)S(1)} %get-tuple-element.57.own_a, bf16[128,512]{1,0:T(8,128)(2,1)S(1)} %collective-permute-done.3.a2, bf16[128,512]{1,0:T(8,128)(2,1)S(1)} %collective-permute-done.4.a1, ...), custom_call_target="tpu_custom_call" | custom-call | flops 1048576 | tf_op jit(solution)/shard_map/pallas_call | solution.py:41
  (39 shorter events, 11.4 us)
Async XLA Ops:
  0.6 20.9 %copy-start.6 = (f32[8]{0:T(128)S(1)}, f32[8]{0:T(128)}, u32[]{:S(2)}) copy-start(f32[8]{0:T(128)} %param.14) | copy-start | bytes 100
  0.6 21.0 %copy-start.2 = (bf16[1024,256]{1,0:T(8,128)(2,1)S(1)}, bf16[1024,256]{1,0:T(8,128)(2,1)}, u32[]{:S(2)}) copy-start(bf16[1024,256]{1,0:T(8,128)(2,1)} %w_out.1) | copy-start | bytes 1572868
  13.5 16.0 %all-to-all-start = ((f32[16,2,1024]{2,1,0:T(2,128)}), f32[16,2,1024]{2,1,0:T(2,128)S(1)}, u32[]{:S(2)}, u32[]{:S(2)}) async-start(f32[16,2,1024]{2,1,0:T(2,128)} %get-tuple-element.39.after), calls=%async_computation | async-start | bytes 262144 | tf_op jit(solution)/shard_map/all_to_all | solution.py:31
  21.7 7.9 %copy-start = (f32[1024]{0:T(1024)S(1)}, f32[1024]{0:T(1024)}, u32[]{:S(2)}) copy-start(f32[1024]{0:T(1024)} %param.10) | copy-start | bytes 12292
  21.7 7.9 %copy-start.1 = (f32[1024]{0:T(1024)S(1)}, f32[1024]{0:T(1024)}, u32[]{:S(2)}) copy-start(f32[1024]{0:T(1024)} %param.11) | copy-start | bytes 12292
  27.3 10.1 %copy-start.3 = (s32[1024]{0:T(1024)S(1)}, s32[1024]{0:T(1024)}, u32[]{:S(2)}) copy-start(s32[1024]{0:T(1024)} %param.15) | copy-start | bytes 12292
  32.9 9.9 %all-to-all-start.1 = ((f32[8,8,128]{2,1,0:T(8,128)}), f32[8,8,128]{2,1,0:T(8,128)S(1)}, u32[]{:S(2)}, u32[]{:S(2)}) async-start(f32[8,8,128]{2,1,0:T(8,128)} %get-tuple-element.43.after), calls=%async_computation.1 | async-start | bytes 65536 | tf_op jit(solution)/shard_map/all_to_all | solution.py:31
  47.1 19.3 %all-to-all-start.2 = ((bf16[16,88,256]{2,1,0:T(8,128)(2,1)}), bf16[16,88,256]{2,1,0:T(8,128)(2,1)S(1)}, u32[]{:S(2)}, u32[]{:S(2)}) async-start(bf16[16,88,256]{2,1,0:T(8,128)(2,1)} %get-tuple-element.48), calls=%async_computation.2 | async-start | bytes 1441792 | tf_op jit(solution)/shard_map/all_to_all | solution.py:31
  69.4 14.2 %copy-start.4 = (bf16[544,512]{1,0:T(8,128)(2,1)S(1)}, bf16[544,512]{1,0:T(8,128)(2,1)}, u32[]{:S(2)}) copy-start(bf16[544,512]{1,0:T(8,128)(2,1)} %get-tuple-element.62) | copy-start | bytes 1671172
  69.4 23.8 %copy-start.5 = (bf16[512,512]{1,0:T(8,128)(2,1)S(1)}, bf16[512,512]{1,0:T(8,128)(2,1)}, u32[]{:S(2)}) copy-start(bf16[512,512]{1,0:T(8,128)(2,1)} %get-tuple-element.54) | copy-start | bytes 1572868
  78.3 14.8 %collective-permute-start.1 = (bf16[512,512]{1,0:T(8,128)(2,1)}, bf16[512,512]{1,0:T(8,128)(2,1)S(1)}, u32[]{:S(2)}, u32[]{:S(2)}) collective-permute-start(bf16[512,512]{1,0:T(8,128)(2,1)} %get-tuple-element.55), channel_id=1, source_target_pairs={{0,32},{32,64},{64,96},{96,0},{1,33},{33,65},{65,97},{97,1},{2,34}... | collective-permute-start | bytes 1572872 | tf_op jit(solution)/shard_map/ppermute | solution.py:27
  80.3 30.6 %collective-permute-start.7 = (bf16[544,512]{1,0:T(8,128)(2,1)}, bf16[544,512]{1,0:T(8,128)(2,1)S(1)}, u32[]{:S(2)}, u32[]{:S(2)}) collective-permute-start(bf16[544,512]{1,0:T(8,128)(2,1)} %get-tuple-element.63), channel_id=1, source_target_pairs={{0,8},{8,16},{16,24},{24,0},{1,9},{9,17},{17,25},{25,1},{2,10},{10... | collective-permute-start | bytes 1671176 | tf_op jit(solution)/shard_map/ppermute | solution.py:27
  81.8 29.1 %collective-permute-start.8 = (bf16[544,512]{1,0:T(8,128)(2,1)}, bf16[544,512]{1,0:T(8,128)(2,1)S(1)}, u32[]{:S(2)}, u32[]{:S(2)}) collective-permute-start(bf16[544,512]{1,0:T(8,128)(2,1)} %get-tuple-element.52.after), channel_id=1, source_target_pairs={{0,24},{8,0},{16,8},{24,16},{1,25},{9,1},{17,9},{25,17},{2,26},{10... | collective-permute-start | bytes 1671176 | tf_op jit(solution)/shard_map/ppermute | solution.py:27
  83.6 27.3 %collective-permute-start.6 = (bf16[544,512]{1,0:T(8,128)(2,1)S(1)}, bf16[544,512]{1,0:T(8,128)(2,1)S(1)}, u32[]{:S(2)}, u32[]{:S(2)}) collective-permute-start(bf16[544,512]{1,0:T(8,128)(2,1)S(1)} %copy-done.4), channel_id=1, source_target_pairs={{0,16},{8,24},{16,0},{24,8},{1,17},{9,25},{17,1},{25,9},{2,18},{10... | collective-permute-start | bytes 1671176 | tf_op jit(solution)/shard_map/ppermute | solution.py:27
  85.3 22.8 %collective-permute-start.2 = (bf16[512,512]{1,0:T(8,128)(2,1)}, bf16[512,512]{1,0:T(8,128)(2,1)S(1)}, u32[]{:S(2)}, u32[]{:S(2)}) collective-permute-start(bf16[512,512]{1,0:T(8,128)(2,1)} %get-tuple-element.56), channel_id=1, source_target_pairs={{0,96},{32,0},{64,32},{96,64},{1,97},{33,1},{65,33},{97,65},{2,98}... | collective-permute-start | bytes 1572872 | tf_op jit(solution)/shard_map/ppermute | solution.py:27
  93.2 15.0 %collective-permute-start = (bf16[512,512]{1,0:T(8,128)(2,1)S(1)}, bf16[512,512]{1,0:T(8,128)(2,1)S(1)}, u32[]{:S(2)}, u32[]{:S(2)}) collective-permute-start(bf16[512,512]{1,0:T(8,128)(2,1)S(1)} %copy-done.5), channel_id=1, source_target_pairs={{0,64},{32,96},{64,0},{96,32},{1,65},{33,97},{65,1},{97,33},{2,66}... | collective-permute-start | bytes 1572872 | tf_op jit(solution)/shard_map/ppermute | solution.py:27
  108.9 8.0 %collective-permute-start.3 = (bf16[128,512]{1,0:T(8,128)(2,1)S(1)}, bf16[128,512]{1,0:T(8,128)(2,1)S(1)}, u32[]{:S(2)}, u32[]{:S(2)}) collective-permute-start(bf16[128,512]{1,0:T(8,128)(2,1)S(1)} %get-tuple-element.58), channel_id=1, source_target_pairs={{0,16},{8,24},{16,0},{24,8},{1,17},{9,25},{17,1},{25,9},{2,18},{10... | collective-permute-start | bytes 393224 | tf_op jit(solution)/shard_map/ppermute | solution.py:27
  111.7 11.0 %collective-permute-start.10 = (bf16[256,512]{1,0:T(8,128)(2,1)S(1)}, bf16[256,512]{1,0:T(8,128)(2,1)S(1)}, u32[]{:S(2)}, u32[]{:S(2)}) collective-permute-start(bf16[256,512]{1,0:T(8,128)(2,1)S(1)} %get-tuple-element.66), channel_id=1, source_target_pairs={{0,32},{32,64},{64,96},{96,0},{1,33},{33,65},{65,97},{97,1},{2,34}... | collective-permute-start | bytes 786440 | tf_op jit(solution)/shard_map/ppermute | solution.py:27
  114.3 8.4 %collective-permute-start.11 = (bf16[256,512]{1,0:T(8,128)(2,1)S(1)}, bf16[256,512]{1,0:T(8,128)(2,1)S(1)}, u32[]{:S(2)}, u32[]{:S(2)}) collective-permute-start(bf16[256,512]{1,0:T(8,128)(2,1)S(1)} %get-tuple-element.67), channel_id=1, source_target_pairs={{0,96},{32,0},{64,32},{96,64},{1,97},{33,1},{65,33},{97,65},{2,98}... | collective-permute-start | bytes 786440 | tf_op jit(solution)/shard_map/ppermute | solution.py:27
  115.1 11.2 %collective-permute-start.9 = (bf16[256,512]{1,0:T(8,128)(2,1)S(1)}, bf16[256,512]{1,0:T(8,128)(2,1)S(1)}, u32[]{:S(2)}, u32[]{:S(2)}) collective-permute-start(bf16[256,512]{1,0:T(8,128)(2,1)S(1)} %get-tuple-element.65.b0), channel_id=1, source_target_pairs={{0,64},{32,96},{64,0},{96,32},{1,65},{33,97},{65,1},{97,33},{2,66}... | collective-permute-start | bytes 786440 | tf_op jit(solution)/shard_map/ppermute | solution.py:27
  116.5 6.2 %collective-permute-start.4 = (bf16[128,512]{1,0:T(8,128)(2,1)S(1)}, bf16[128,512]{1,0:T(8,128)(2,1)S(1)}, u32[]{:S(2)}, u32[]{:S(2)}) collective-permute-start(bf16[128,512]{1,0:T(8,128)(2,1)S(1)} %get-tuple-element.59), channel_id=1, source_target_pairs={{0,8},{8,16},{16,24},{24,0},{1,9},{9,17},{17,25},{25,1},{2,10},{10... | collective-permute-start | bytes 393224 | tf_op jit(solution)/shard_map/ppermute | solution.py:27
  117.0 5.8 %collective-permute-start.5 = (bf16[128,512]{1,0:T(8,128)(2,1)S(1)}, bf16[128,512]{1,0:T(8,128)(2,1)S(1)}, u32[]{:S(2)}, u32[]{:S(2)}) collective-permute-start(bf16[128,512]{1,0:T(8,128)(2,1)S(1)} %get-tuple-element.60), channel_id=1, source_target_pairs={{0,24},{8,0},{16,8},{24,16},{1,25},{9,1},{17,9},{25,17},{2,26},{10... | collective-permute-start | bytes 393224 | tf_op jit(solution)/shard_map/ppermute | solution.py:27

commit v2 on v1

--- a/solution.py
+++ b/solution.py
@@ -66,8 +66,8 @@
     return (codes.astype(F32) * (2.0 / (buckets - 1.0)) - 1.0).astype(BF16)
 
 
-def decode_body(codes_hbm, w_hbm, hidden_hbm, slope_hbm, sums, base, codes, weights, hidden, slope, inputs, pre_a, pre_b, kept,
-                totals, code_sem, w_sem, out_sem):
+def decode_body(codes_hbm, w_hbm, hidden_hbm, slope_hbm, sums_hbm, base, codes, weights, hidden, slope, inputs, pre_a, pre_b, kept,
+                totals, sums, code_sem, w_sem, out_sem, sum_sem):
     rows, units = hidden.shape
     block, tile = pre_a.shape
     blocks, tiles = rows // block, units // tile
@@ -152,6 +152,9 @@
     for k in range(sums.shape[0]):
         sums[k, 0:1, :] = first
         sums[k, 1:2, :] = second
+    put_sums = pltpu.make_async_copy(sums, sums_hbm, sum_sem.at[0])
+    put_sums.start()
+    put_sums.wait()
     for i in range(blocks):
         for k in range(2):
             put(k, i).wait()
@@ -449,24 +452,15 @@
     out[0:rows, :] = dot(left, grad_pre[:, axis * wide : (axis + 1) * wide]).astype(BF16)
 
 
-def near_body(chunks, grads, hidden_hbm, spread_hbm, slope_hbm, coef, both, turned_hbm, piece, grad_pre, grad_gain, grad_bias,
-              loss, z1_hbm, x1_hbm, z3_hbm, x3_hbm, hidden, spread, slope, turned, lines, z1, x1, z3, x3, sem,
-              turned_sem, out_sem):
+def back_body(grads, hidden_hbm, spread_hbm, slope_hbm, coef, both, grad_pre, grad_gain, grad_bias, loss, hidden, spread, slope,
+              sem):
     rows, units = hidden.shape
     block = LANES
     blocks = rows // block
-    parts = turned_sem.shape[0]
-
-    def turn_in(i):
-        at = span(i, turned.shape[0] // parts)
-        return pltpu.make_async_copy(turned_hbm.at[at, :], turned.at[at, :], turned_sem.at[i])
-
     for i in range(blocks):
         rows_in(hidden_hbm, hidden, sem, 0, i, block).start()
         rows_in(spread_hbm, spread, sem, 1, i, block).start()
         rows_in(slope_hbm, slope, sem, 2, i, block).start()
-    for i in range(parts):
-        turn_in(i).start()
     grad_bias[...] = both[2:3, :]
     grad_gain[...] = both[3:4, :]
     loss[...] = both[4:5, 0:LANES]
@@ -485,31 +479,26 @@
         return carry
 
     lax.fori_loop(0, blocks, step, 0)
-    for i in range(parts):
-        turn_in(i).wait()
-    jobs = ((0, 1, z1, z1_hbm), (1, 1, x1, x1_hbm), (0, 3, z3, z3_hbm), (1, 3, x3, x3_hbm))
-
-    def put(k):
-        return pltpu.make_async_copy(jobs[k][2], jobs[k][3], out_sem.at[k])
-
-    for k, (axis, step_on, held, _) in enumerate(jobs):
-        product(axis, chunks[4 * axis + step_on], turned, grad_pre, piece, lines, held)
-        put(k).start()
-    for k in range(len(jobs)):
-        put(k).wait()
-
-
-def own_body(chunks, turned_hbm, grad_pre, piece, after, z0, x0, left, sem):
+
+
+def near_body(step_on, chunks, turned, grad_pre, piece, after, z_hbm, x_hbm, lines, z, x, out_sem):
     del after
-    copies = lefts(turned_hbm, left, sem, chunks[0], chunks[4])
-    for copy in copies:
-        copy.start()
-    rows, wide = z0.shape
-    lay_piece(x0, piece, rows)
-    for copy in copies:
-        copy.wait()
-    for axis, out in ((0, z0), (1, x0)):
-        out[0:rows, :] = dot(left[axis], grad_pre[:, axis * wide : (axis + 1) * wide]).astype(BF16)
+    jobs = ((z, z_hbm), (x, x_hbm))
+
+    def put(axis):
+        return pltpu.make_async_copy(*jobs[axis], out_sem.at[axis])
+
+    for axis in range(2):
+        product(axis, chunks[4 * axis + step_on], turned, grad_pre, piece, lines, jobs[axis][0])
+        put(axis).start()
+    for axis in range(2):
+        put(axis).wait()
+
+
+def own_body(chunks, turned, grad_pre, piece, after, z0, x0, lines):
+    del after
+    product(0, chunks[0], turned, grad_pre, piece, lines, z0)
+    product(1, chunks[4], turned, grad_pre, piece, lines, x0)
 
 
 def middle_body(chunk, own, far, up, down, own_out, far_out, up_out, down_out):
@@ -566,7 +555,7 @@
     hidden, slope, sums, base = call(
         decode_body,
         [(hash_codes, "h"), (w_hash, "h")],
-        [((rows, units), BF16, "h"), ((rows, units), BF16, "h"), ((dp, 2, units), F32, "v"), ((1, units), F32, "v")],
+        [((rows, units), BF16, "h"), ((rows, units), BF16, "h"), ((dp, 2, units), F32, "h"), ((1, units), F32, "v")],
         [
             pltpu.VMEM((rows, codes), jnp.int32),
             pltpu.VMEM((codes, units), BF16),
@@ -577,9 +566,11 @@
             pltpu.VMEM((256, units // 2), F32),
             pltpu.VMEM((256, units), F32),
             pltpu.VMEM((16, units), F32),
+            pltpu.VMEM((dp, 2, units), F32),
             dma((rows // 256,)),
             dma((2,)),
             dma((2, rows // 256)),
+            dma((1,)),
         ],
         flops=2 * rows * codes * units,
         limit=40,
@@ -680,39 +671,37 @@
         limit=10,
         flops=8 * rows * units,
     )
-    near = call(
-        near_body,
-        [
-            (chunks, "s"),
-            (grads, "v"),
-            (hidden, "h"),
-            (spread, "h"),
-            (slope, "h"),
-            (coef, "v"),
-            (both, "p"),
-            (turned, "h"),
-            (piece, "p"),
-        ],
-        [((rows, units), BF16, "p"), ((1, units), F32, "v"), ((1, units), F32, "v"), ((1, LANES), F32, "v")]
-        + [(size, BF16, "h") for size in sizes * 2],
-        [pltpu.VMEM((rows, units), BF16)] * 3
-        + [pltpu.VMEM((codes, rows), BF16), pltpu.VMEM((codes // 4, rows), BF16)]
-        + [pltpu.VMEM(size, BF16) for size in sizes * 2]
-        + [dma((3, lines)), dma((4,)), dma((4,))],
+    grad_pre, grad_gain, grad_bias, loss = call(
+        back_body,
+        [(grads, "v"), (hidden, "h"), (spread, "h"), (slope, "h"), (coef, "v"), (both, "p")],
+        [((rows, units), BF16, "p"), ((1, units), F32, "v"), ((1, units), F32, "v"), ((1, LANES), F32, "v")],
+        [pltpu.VMEM((rows, units), BF16)] * 3 + [dma((3, lines))],
         limit=20,
-        flops=2 * rows * half * codes,
-    )
-    grad_pre, grad_gain, grad_bias, loss = near[:4]
+        flops=8 * rows * units,
+    )
+
+    def near(step_on, after):
+        return call(
+            functools.partial(near_body, step_on),
+            [(chunks, "s"), (turned, "p"), (grad_pre, "p"), (piece, "p"), (after, "h")],
+            [(size, BF16, "h") for size in sizes],
+            [pltpu.VMEM((codes // 4, rows), BF16)] + [pltpu.VMEM(size, BF16) for size in sizes] + [dma((2,))],
+            flops=rows * half * codes,
+            limit=8,
+        )
+
+    up = near(1, terms)
+    down = near(3, up[0])
     own_z, own_x = call(
         own_body,
-        [(chunks, "s"), (turned, "h"), (grad_pre, "p"), (piece, "p"), (near[7], "h")],
+        [(chunks, "s"), (turned, "p"), (grad_pre, "p"), (piece, "p"), (down[0], "h")],
         [(size, BF16, "p") for size in sizes],
-        [pltpu.VMEM((2, codes // 4, rows), BF16), dma((5,))],
-        limit=6,
+        [pltpu.VMEM((codes // 4, rows), BF16)],
+        limit=4,
         flops=rows * half * codes,
     )
     made = {("z", 2): far_z, ("x", 2): far_x, ("z", 0): own_z, ("x", 0): own_x}
-    made.update(zip((("z", 1), ("x", 1), ("z", 3), ("x", 3)), near[4:]))
+    made.update(zip((("z", 1), ("x", 1), ("z", 3), ("x", 3)), (*up, *down)))
     got = {(axis, step): hop(made[axis, step], axis, step) for step in (2, 1, 3) for axis in DP}
     other = {"z": "x", "x": "z"}
     last = []

time: 129 us -> 130 us (level)
  Pallas kernels: 59 us -> 56.9 us
  waiting for transfers between devices: 29.7 us -> 31 us
    pallas_call x12 -> x14, Pallas kernels: 59 us -> 56.9 us  [call(): pl.pallas_call(body, out_shape=shapes, in_specs=[pl.BlockSpec(memory_spac...]
    ppermute x12, starting transfers between devices: 20.7 us -> 22 us  [hop(): lax.ppermute(value, axis, [(i, (i + step) % count) for i in range(count)])]
  transfers between devices with their start and end apart: 15 -> 15, of which waited for: 6 -> 8; matrix products, arithmetic and copies ran while one was open for 0% -> 0% of each run, Pallas kernels for 19% -> 20%
where the time goes in v2:
time: 130 us; the launch traced here: 129 us
  Pallas kernels  56.9 us (44%)
  starting transfers between devices  39.5 us (30%)
  waiting for transfers between devices  31 us (24%)
    pallas_call x14, Pallas kernels, call(): pl.pallas_call(body, out_shape=shapes, in_specs=[pl.BlockSpec(memory_spac...  56.9 us
    ppermute x12, waiting for transfers between devices, hop(): lax.ppermute(value, axis, [(i, (i + step) % count) for i in range(count)])  23.4 us
    ppermute x12, starting transfers between devices, hop(): lax.ppermute(value, axis, [(i, (i + step) % count) for i in range(count)])  22 us
    all_to_all x3, starting transfers between devices, exchange(): return lax.all_to_all(blocks, axes, 0, 0, tiled=True)  17.5 us
    all_to_all x3, waiting for transfers between devices, exchange(): return lax.all_to_all(blocks, axes, 0, 0, tiled=True)  7.54 us
  transfers between devices with their start and end apart: 15, of which 8 were waited for; matrix products, arithmetic and copies ran while one was open for 0% of the time, Pallas kernels for 20%

profile of v2, /device:TPU:0, one launch (start us, length us, event | category | flops | bytes accessed | tf_op | source)
XLA Modules:
  0.0 129.1 jit_solution(9013523595686984265)
XLA Ops:
  0.7 12.3 %shard_map.119 = (bf16[1024,1024]{1,0:T(8,128)(2,1)}, bf16[1024,1024]{1,0:T(8,128)(2,1)}, f32[16,2,1024]{2,1,0:T(2,128)}, f32[1,1024]{1,0:T(1,128)S(1)}) custom-call(s32[1024,2048]{1,0:T(8,128)} %codes_hbm.3, bf16[2048,1024]{1,0:T(8,128)(2,1)} %w_hbm.1), custom_call_target="tpu_custom_call" | custom-call | flops 4294967296 | tf_op jit(solution)/shard_map/pallas_call | solution.py:41
  12.9 8.0 %all-to-all-start = ((f32[16,2,1024]{2,1,0:T(2,128)}), f32[16,2,1024]{2,1,0:T(2,128)S(1)}, u32[]{:S(2)}, u32[]{:S(2)}) async-start(f32[16,2,1024]{2,1,0:T(2,128)} %get-tuple-element.39.after), calls=%async_computation | async-start | bytes 262144 | tf_op jit(solution)/shard_map/all_to_all | solution.py:31
  21.1 5.6 %shard_map.120 = (bf16[1024,1024]{1,0:T(8,128)(2,1)}, f32[256,1024]{1,0:T(8,128)S(1)}) custom-call(f32[16,2,1024]{2,1,0:T(2,128)} %get-tuple-element.39.after, bf16[8192,256]{1,0:T(8,128)(2,1)} %bitcast.21, f32[1,512]{1,0:T(1,128)S(1)} %reshape_tile.3.mix, bf16[1024,256]{1,0:T(8,128)(2,1)S(1)} %copy-done.3), custom_call_target="tpu_custom_call" | custom-call | flops 2147483648 | tf_op jit(solution)/shard_map/pallas_call | solution.py:41
  28.9 3.4 %shard_map.121 = (f32[8,1024]{1,0:T(8,128)S(1)}, f32[8,8,128]{2,1,0:T(8,128)}) custom-call(f32[16,2,1024]{2,1,0:T(2,128)S(1)} %all-to-all-done.arrived, f32[1,1024]{1,0:T(1,128)S(1)} %bitcast.19, f32[1,1024]{1,0:T(1,128)S(1)} %bitcast.20, f32[1,1024]{1,0:T(1,128)S(1)} %get-tuple-element.40.base, bf16[1024,1024]{1,0:T(8,128)(2,1)} %get-tuple-element.41.hidden_hbm, ...), custom_call_target="tpu_custom_call" | custom-call | flops 4194304 | tf_op jit(solution)/shard_map/pallas_call | solution.py:41
  32.3 4.5 %all-to-all-start.1 = ((f32[8,8,128]{2,1,0:T(8,128)}), f32[8,8,128]{2,1,0:T(8,128)S(1)}, u32[]{:S(2)}, u32[]{:S(2)}) async-start(f32[8,8,128]{2,1,0:T(8,128)} %get-tuple-element.43.after), calls=%async_computation.1 | async-start | bytes 65536 | tf_op jit(solution)/shard_map/all_to_all | solution.py:31
  36.9 5.3 %all-to-all-done.1.arrived = f32[8,8,128]{2,1,0:T(8,128)S(1)} async-done(((f32[8,8,128]{2,1,0:T(8,128)}), f32[8,8,128]{2,1,0:T(8,128)S(1)}, u32[]{:S(2)}, u32[]{:S(2)}) %all-to-all-start.1) | async-done | bytes 32800 | tf_op jit(solution)/shard_map/all_to_all | solution.py:31
  42.3 4.2 %shard_map.123 = (f32[8,128]{1,0:T(8,128)S(1)}, bf16[16,88,256]{2,1,0:T(8,128)(2,1)}) custom-call(f32[8,8,128]{2,1,0:T(8,128)S(1)} %all-to-all-done.1.arrived, f32[8,128]{1,0:T(8,128)S(1)} %convert_bitcast_fusion.labels, bf16[1024,1024]{1,0:T(8,128)(2,1)} %get-tuple-element.41.hidden_hbm, bf16[1024,1024]{1,0:T(8,128)(2,1)} %get-tuple-element.42.spread_hbm, ...), custom_call_target="tpu_custom_call" | custom-call | flops 536870912 | tf_op jit(solution)/shard_map/pallas_call | solution.py:41
  46.5 5.1 %all-to-all-start.2 = ((bf16[16,88,256]{2,1,0:T(8,128)(2,1)}), bf16[16,88,256]{2,1,0:T(8,128)(2,1)S(1)}, u32[]{:S(2)}, u32[]{:S(2)}) async-start(bf16[16,88,256]{2,1,0:T(8,128)(2,1)} %get-tuple-element.48), calls=%async_computation.2 | async-start | bytes 1441792 | tf_op jit(solution)/shard_map/all_to_all | solution.py:31
  51.6 5.5 %shard_map.122.turned_hbm.turned = bf16[2048,1024]{1,0:T(8,128)(2,1)} custom-call(s32[1024,2048]{1,0:T(8,128)} %codes_hbm.3, f32[8,8,128]{2,1,0:T(8,128)} %get-tuple-element.43.after), custom_call_target="tpu_custom_call" | custom-call | flops 4294967296 | tf_op jit(solution)/shard_map/pallas_call | solution.py:41
  57.2 8.6 %shard_map.124.terms_hbm.after = bf16[6,512,512]{2,1,0:T(8,128)(2,1)} custom-call(s32[8]{0:T(128)S(1)} %stack.56.chunks, f32[8,128]{1,0:T(8,128)S(1)} %get-tuple-element.46.grads, bf16[1024,1024]{1,0:T(8,128)(2,1)} %get-tuple-element.41.hidden_hbm, bf16[1024,1024]{1,0:T(8,128)(2,1)} %get-tuple-element.42.spread_hbm, ...), custom_call_target="tpu_custom_call" | custom-call | flops 6442450944 | tf_op jit(solution)/shard_map/pallas_call | solution.py:41
  65.8 3.0 %shard_map.125 = (bf16[512,512]{1,0:T(8,128)(2,1)}, bf16[544,512]{1,0:T(8,128)(2,1)}, f32[8,1024]{1,0:T(8,128)S(1)}, bf16[64,256]{1,0:T(8,128)(2,1)S(1)}) custom-call(bf16[16,88,256]{2,1,0:T(8,128)(2,1)S(1)} %all-to-all-done.2.arrived, f32[8,1024]{1,0:T(8,128)S(1)} %get-tuple-element.44.coef, bf16[6,512,512]{2,1,0:T(8,128)(2,1)} %shard_map.124.terms_hbm.after), custom_call_target="tpu_custom_call" | custom-call | flops 8388608 | tf_op jit(solution)/shard_map/pallas_call | solution.py:41
  68.8 3.8 %shard_map.126 = (bf16[1024,1024]{1,0:T(8,128)(2,1)S(1)}, f32[1,1024]{1,0:T(1,128)}, f32[1,1024]{1,0:T(1,128)}, f32[1,128]{1,0:T(1,128)}) custom-call(f32[8,128]{1,0:T(8,128)S(1)} %get-tuple-element.46.grads, bf16[1024,1024]{1,0:T(8,128)(2,1)} %get-tuple-element.41.hidden_hbm, bf16[1024,1024]{1,0:T(8,128)(2,1)} %get-tuple-element.42.spread_hbm, ...), custom_call_target="tpu_custom_call" | custom-call | flops 8388608 | tf_op jit(solution)/shard_map/pallas_call | solution.py:41
  72.8 2.6 %shard_map.127 = (bf16[512,512]{1,0:T(8,128)(2,1)}, bf16[544,512]{1,0:T(8,128)(2,1)}) custom-call(s32[8]{0:T(128)S(1)} %stack.56.chunks, bf16[2048,1024]{1,0:T(8,128)(2,1)S(1)} %copy-done, bf16[1024,1024]{1,0:T(8,128)(2,1)S(1)} %get-tuple-element.50.grad_pre, bf16[64,256]{1,0:T(8,128)(2,1)S(1)} %get-tuple-element.51.piece, ...), custom_call_target="tpu_custom_call" | custom-call | flops 1073741824 | tf_op jit(solution)/shard_map/pallas_call | solution.py:41
  78.9 2.6 %shard_map.128 = (bf16[512,512]{1,0:T(8,128)(2,1)}, bf16[544,512]{1,0:T(8,128)(2,1)}) custom-call(s32[8]{0:T(128)S(1)} %stack.56.chunks, bf16[2048,1024]{1,0:T(8,128)(2,1)S(1)} %copy-done, bf16[1024,1024]{1,0:T(8,128)(2,1)S(1)} %get-tuple-element.50.grad_pre, bf16[64,256]{1,0:T(8,128)(2,1)S(1)} %get-tuple-element.51.piece, ...), custom_call_target="tpu_custom_call" | custom-call | flops 1073741824 | tf_op jit(solution)/shard_map/pallas_call | solution.py:41
  81.6 2.8 %collective-permute-start.6 = (bf16[544,512]{1,0:T(8,128)(2,1)S(1)}, bf16[544,512]{1,0:T(8,128)(2,1)S(1)}, u32[]{:S(2)}, u32[]{:S(2)}) collective-permute-start(bf16[544,512]{1,0:T(8,128)(2,1)S(1)} %copy-done.5), channel_id=1, source_target_pairs={{0,16},{8,24},{16,0},{24,8},{1,17},{9,25},{17,1},{25,9},{2,18},{10... | collective-permute-start | bytes 1671176 | tf_op jit(solution)/shard_map/ppermute | solution.py:27
  85.8 2.7 %collective-permute-start = (bf16[512,512]{1,0:T(8,128)(2,1)S(1)}, bf16[512,512]{1,0:T(8,128)(2,1)S(1)}, u32[]{:S(2)}, u32[]{:S(2)}) collective-permute-start(bf16[512,512]{1,0:T(8,128)(2,1)S(1)} %copy-done.6), channel_id=1, source_target_pairs={{0,64},{32,96},{64,0},{96,32},{1,65},{33,97},{65,1},{97,33},{2,66}... | collective-permute-start | bytes 1572872 | tf_op jit(solution)/shard_map/ppermute | solution.py:27
  88.5 2.5 %collective-permute-done.1.up = bf16[512,512]{1,0:T(8,128)(2,1)S(1)} collective-permute-done((bf16[512,512]{1,0:T(8,128)(2,1)}, bf16[512,512]{1,0:T(8,128)(2,1)S(1)}, u32[]{:S(2)}, u32[]{:S(2)}) %collective-permute-start.1) | collective-permute-done | bytes 524320 | tf_op jit(solution)/shard_map/ppermute | solution.py:27
  90.9 2.7 %collective-permute-start.2 = (bf16[512,512]{1,0:T(8,128)(2,1)}, bf16[512,512]{1,0:T(8,128)(2,1)S(1)}, u32[]{:S(2)}, u32[]{:S(2)}) collective-permute-start(bf16[512,512]{1,0:T(8,128)(2,1)} %get-tuple-element.53.after), channel_id=1, source_target_pairs={{0,96},{32,0},{64,32},{96,64},{1,97},{33,1},{65,33},{97,65},{2,98}... | collective-permute-start | bytes 1572872 | tf_op jit(solution)/shard_map/ppermute | solution.py:27
  95.6 7.0 %collective-permute-done.far = bf16[512,512]{1,0:T(8,128)(2,1)S(1)} collective-permute-done((bf16[512,512]{1,0:T(8,128)(2,1)S(1)}, bf16[512,512]{1,0:T(8,128)(2,1)S(1)}, u32[]{:S(2)}, u32[]{:S(2)}) %collective-permute-start) | collective-permute-done | bytes 524320 | tf_op jit(solution)/shard_map/ppermute | solution.py:27
  102.6 7.0 %collective-permute-done.2.down = bf16[512,512]{1,0:T(8,128)(2,1)S(1)} collective-permute-done((bf16[512,512]{1,0:T(8,128)(2,1)}, bf16[512,512]{1,0:T(8,128)(2,1)S(1)}, u32[]{:S(2)}, u32[]{:S(2)}) %collective-permute-start.2) | collective-permute-done | bytes 524320 | tf_op jit(solution)/shard_map/ppermute | solution.py:27
  111.7 2.6 %collective-permute-start.10 = (bf16[256,512]{1,0:T(8,128)(2,1)S(1)}, bf16[256,512]{1,0:T(8,128)(2,1)S(1)}, u32[]{:S(2)}, u32[]{:S(2)}) collective-permute-start(bf16[256,512]{1,0:T(8,128)(2,1)S(1)} %get-tuple-element.66), channel_id=1, source_target_pairs={{0,32},{32,64},{64,96},{96,0},{1,33},{33,65},{65,97},{97,1},{2,34}... | collective-permute-start | bytes 786440 | tf_op jit(solution)/shard_map/ppermute | solution.py:27
  117.5 2.7 %collective-permute-start.5 = (bf16[128,512]{1,0:T(8,128)(2,1)S(1)}, bf16[128,512]{1,0:T(8,128)(2,1)S(1)}, u32[]{:S(2)}, u32[]{:S(2)}) collective-permute-start(bf16[128,512]{1,0:T(8,128)(2,1)S(1)} %get-tuple-element.59), channel_id=1, source_target_pairs={{0,24},{8,0},{16,8},{24,16},{1,25},{9,1},{17,9},{25,17},{2,26},{10... | collective-permute-start | bytes 393224 | tf_op jit(solution)/shard_map/ppermute | solution.py:27
  120.2 2.9 %collective-permute-done.4.a1 = bf16[128,512]{1,0:T(8,128)(2,1)S(1)} collective-permute-done((bf16[128,512]{1,0:T(8,128)(2,1)S(1)}, bf16[128,512]{1,0:T(8,128)(2,1)S(1)}, u32[]{:S(2)}, u32[]{:S(2)}) %collective-permute-start.4) | collective-permute-done | bytes 131104 | tf_op jit(solution)/shard_map/ppermute | solution.py:27
  123.4 3.7 %collective-permute-done.9.b2 = bf16[256,512]{1,0:T(8,128)(2,1)S(1)} collective-permute-done((bf16[256,512]{1,0:T(8,128)(2,1)S(1)}, bf16[256,512]{1,0:T(8,128)(2,1)S(1)}, u32[]{:S(2)}, u32[]{:S(2)}) %collective-permute-start.9) | collective-permute-done | bytes 262176 | tf_op jit(solution)/shard_map/ppermute | solution.py:27
  (43 shorter events, 16.9 us)
Async XLA Ops:
  0.6 20.3 %copy-start.7 = (f32[8]{0:T(128)S(1)}, f32[8]{0:T(128)}, u32[]{:S(2)}) copy-start(f32[8]{0:T(128)} %param.14) | copy-start | bytes 100
  0.6 20.4 %copy-start.3 = (bf16[1024,256]{1,0:T(8,128)(2,1)S(1)}, bf16[1024,256]{1,0:T(8,128)(2,1)}, u32[]{:S(2)}) copy-start(bf16[1024,256]{1,0:T(8,128)(2,1)} %w_out.1) | copy-start | bytes 1572868
  12.9 16.0 %all-to-all-start = ((f32[16,2,1024]{2,1,0:T(2,128)}), f32[16,2,1024]{2,1,0:T(2,128)S(1)}, u32[]{:S(2)}, u32[]{:S(2)}) async-start(f32[16,2,1024]{2,1,0:T(2,128)} %get-tuple-element.39.after), calls=%async_computation | async-start | bytes 262144 | tf_op jit(solution)/shard_map/all_to_all | solution.py:31
  21.1 7.9 %copy-start.1 = (f32[1024]{0:T(1024)S(1)}, f32[1024]{0:T(1024)}, u32[]{:S(2)}) copy-start(f32[1024]{0:T(1024)} %param.10) | copy-start | bytes 12292
  21.1 7.9 %copy-start.2 = (f32[1024]{0:T(1024)S(1)}, f32[1024]{0:T(1024)}, u32[]{:S(2)}) copy-start(f32[1024]{0:T(1024)} %param.11) | copy-start | bytes 12292
  26.7 10.1 %copy-start.4 = (s32[1024]{0:T(1024)S(1)}, s32[1024]{0:T(1024)}, u32[]{:S(2)}) copy-start(s32[1024]{0:T(1024)} %param.15) | copy-start | bytes 12292
  32.3 9.9 %all-to-all-start.1 = ((f32[8,8,128]{2,1,0:T(8,128)}), f32[8,8,128]{2,1,0:T(8,128)S(1)}, u32[]{:S(2)}, u32[]{:S(2)}) async-start(f32[8,8,128]{2,1,0:T(8,128)} %get-tuple-element.43.after), calls=%async_computation.1 | async-start | bytes 65536 | tf_op jit(solution)/shard_map/all_to_all | solution.py:31
  46.5 19.2 %all-to-all-start.2 = ((bf16[16,88,256]{2,1,0:T(8,128)(2,1)}), bf16[16,88,256]{2,1,0:T(8,128)(2,1)S(1)}, u32[]{:S(2)}, u32[]{:S(2)}) async-start(bf16[16,88,256]{2,1,0:T(8,128)(2,1)} %get-tuple-element.48), calls=%async_computation.2 | async-start | bytes 1441792 | tf_op jit(solution)/shard_map/all_to_all | solution.py:31
  68.8 4.1 %copy-start = (bf16[2048,1024]{1,0:T(8,128)(2,1)S(1)}, bf16[2048,1024]{1,0:T(8,128)(2,1)}, u32[]{:S(2)}) copy-start(bf16[2048,1024]{1,0:T(8,128)(2,1)} %shard_map.122.turned_hbm.turned) | copy-start | bytes 12582916
  75.5 15.5 %collective-permute-start.1 = (bf16[512,512]{1,0:T(8,128)(2,1)}, bf16[512,512]{1,0:T(8,128)(2,1)S(1)}, u32[]{:S(2)}, u32[]{:S(2)}) collective-permute-start(bf16[512,512]{1,0:T(8,128)(2,1)} %get-tuple-element.52.after), channel_id=1, source_target_pairs={{0,32},{32,64},{64,96},{96,0},{1,33},{33,65},{65,97},{97,1},{2,34}... | collective-permute-start | bytes 1572872 | tf_op jit(solution)/shard_map/ppermute | solution.py:27
  77.4 4.1 %copy-start.5 = (bf16[544,512]{1,0:T(8,128)(2,1)S(1)}, bf16[544,512]{1,0:T(8,128)(2,1)}, u32[]{:S(2)}) copy-start(bf16[544,512]{1,0:T(8,128)(2,1)} %get-tuple-element.61) | copy-start | bytes 1671172
  77.4 8.3 %copy-start.6 = (bf16[512,512]{1,0:T(8,128)(2,1)S(1)}, bf16[512,512]{1,0:T(8,128)(2,1)}, u32[]{:S(2)}) copy-start(bf16[512,512]{1,0:T(8,128)(2,1)} %get-tuple-element.55) | copy-start | bytes 1572868
  77.4 33.4 %collective-permute-start.7 = (bf16[544,512]{1,0:T(8,128)(2,1)}, bf16[544,512]{1,0:T(8,128)(2,1)S(1)}, u32[]{:S(2)}, u32[]{:S(2)}) collective-permute-start(bf16[544,512]{1,0:T(8,128)(2,1)} %get-tuple-element.62), channel_id=1, source_target_pairs={{0,8},{8,16},{16,24},{24,0},{1,9},{9,17},{17,25},{25,1},{2,10},{10... | collective-permute-start | bytes 1671176 | tf_op jit(solution)/shard_map/ppermute | solution.py:27
  81.6 29.3 %collective-permute-start.6 = (bf16[544,512]{1,0:T(8,128)(2,1)S(1)}, bf16[544,512]{1,0:T(8,128)(2,1)S(1)}, u32[]{:S(2)}, u32[]{:S(2)}) collective-permute-start(bf16[544,512]{1,0:T(8,128)(2,1)S(1)} %copy-done.5), channel_id=1, source_target_pairs={{0,16},{8,24},{16,0},{24,8},{1,17},{9,25},{17,1},{25,9},{2,18},{10... | collective-permute-start | bytes 1671176 | tf_op jit(solution)/shard_map/ppermute | solution.py:27
  84.3 26.5 %collective-permute-start.8 = (bf16[544,512]{1,0:T(8,128)(2,1)}, bf16[544,512]{1,0:T(8,128)(2,1)S(1)}, u32[]{:S(2)}, u32[]{:S(2)}) collective-permute-start(bf16[544,512]{1,0:T(8,128)(2,1)} %get-tuple-element.63), channel_id=1, source_target_pairs={{0,24},{8,0},{16,8},{24,16},{1,25},{9,1},{17,9},{25,17},{2,26},{10... | collective-permute-start | bytes 1671176 | tf_op jit(solution)/shard_map/ppermute | solution.py:27
  85.8 16.8 %collective-permute-start = (bf16[512,512]{1,0:T(8,128)(2,1)S(1)}, bf16[512,512]{1,0:T(8,128)(2,1)S(1)}, u32[]{:S(2)}, u32[]{:S(2)}) collective-permute-start(bf16[512,512]{1,0:T(8,128)(2,1)S(1)} %copy-done.6), channel_id=1, source_target_pairs={{0,64},{32,96},{64,0},{96,32},{1,65},{33,97},{65,1},{97,33},{2,66}... | collective-permute-start | bytes 1572872 | tf_op jit(solution)/shard_map/ppermute | solution.py:27
  90.9 18.6 %collective-permute-start.2 = (bf16[512,512]{1,0:T(8,128)(2,1)}, bf16[512,512]{1,0:T(8,128)(2,1)S(1)}, u32[]{:S(2)}, u32[]{:S(2)}) collective-permute-start(bf16[512,512]{1,0:T(8,128)(2,1)} %get-tuple-element.53.after), channel_id=1, source_target_pairs={{0,96},{32,0},{64,32},{96,64},{1,97},{33,1},{65,33},{97,65},{2,98}... | collective-permute-start | bytes 1572872 | tf_op jit(solution)/shard_map/ppermute | solution.py:27
  110.4 7.1 %collective-permute-start.3 = (bf16[128,512]{1,0:T(8,128)(2,1)S(1)}, bf16[128,512]{1,0:T(8,128)(2,1)S(1)}, u32[]{:S(2)}, u32[]{:S(2)}) collective-permute-start(bf16[128,512]{1,0:T(8,128)(2,1)S(1)} %get-tuple-element.57), channel_id=1, source_target_pairs={{0,16},{8,24},{16,0},{24,8},{1,17},{9,25},{17,1},{25,9},{2,18},{10... | collective-permute-start | bytes 393224 | tf_op jit(solution)/shard_map/ppermute | solution.py:27
  111.7 11.5 %collective-permute-start.10 = (bf16[256,512]{1,0:T(8,128)(2,1)S(1)}, bf16[256,512]{1,0:T(8,128)(2,1)S(1)}, u32[]{:S(2)}, u32[]{:S(2)}) collective-permute-start(bf16[256,512]{1,0:T(8,128)(2,1)S(1)} %get-tuple-element.66), channel_id=1, source_target_pairs={{0,32},{32,64},{64,96},{96,0},{1,33},{33,65},{65,97},{97,1},{2,34}... | collective-permute-start | bytes 786440 | tf_op jit(solution)/shard_map/ppermute | solution.py:27
  114.3 9.2 %collective-permute-start.11 = (bf16[256,512]{1,0:T(8,128)(2,1)S(1)}, bf16[256,512]{1,0:T(8,128)(2,1)S(1)}, u32[]{:S(2)}, u32[]{:S(2)}) collective-permute-start(bf16[256,512]{1,0:T(8,128)(2,1)S(1)} %get-tuple-element.67), channel_id=1, source_target_pairs={{0,96},{32,0},{64,32},{96,64},{1,97},{33,1},{65,33},{97,65},{2,98}... | collective-permute-start | bytes 786440 | tf_op jit(solution)/shard_map/ppermute | solution.py:27
  115.0 12.2 %collective-permute-start.9 = (bf16[256,512]{1,0:T(8,128)(2,1)S(1)}, bf16[256,512]{1,0:T(8,128)(2,1)S(1)}, u32[]{:S(2)}, u32[]{:S(2)}) collective-permute-start(bf16[256,512]{1,0:T(8,128)(2,1)S(1)} %get-tuple-element.65.b0), channel_id=1, source_target_pairs={{0,64},{32,96},{64,0},{96,32},{1,65},{33,97},{65,1},{97,33},{2,66}... | collective-permute-start | bytes 786440 | tf_op jit(solution)/shard_map/ppermute | solution.py:27
  116.9 6.2 %collective-permute-start.4 = (bf16[128,512]{1,0:T(8,128)(2,1)S(1)}, bf16[128,512]{1,0:T(8,128)(2,1)S(1)}, u32[]{:S(2)}, u32[]{:S(2)}) collective-permute-start(bf16[128,512]{1,0:T(8,128)(2,1)S(1)} %get-tuple-element.58), channel_id=1, source_target_pairs={{0,8},{8,16},{16,24},{24,0},{1,9},{9,17},{17,25},{25,1},{2,10},{10... | collective-permute-start | bytes 393224 | tf_op jit(solution)/shard_map/ppermute | solution.py:27
  117.5 5.6 %collective-permute-start.5 = (bf16[128,512]{1,0:T(8,128)(2,1)S(1)}, bf16[128,512]{1,0:T(8,128)(2,1)S(1)}, u32[]{:S(2)}, u32[]{:S(2)}) collective-permute-start(bf16[128,512]{1,0:T(8,128)(2,1)S(1)} %get-tuple-element.59), channel_id=1, source_target_pairs={{0,24},{8,0},{16,8},{24,16},{1,25},{9,1},{17,9},{25,17},{2,26},{10... | collective-permute-start | bytes 393224 | tf_op jit(solution)/shard_map/ppermute | solution.py:27
